TPU v7x, 32 devices: a whole 2x2x4 slice. The times are simulated.
32 devices in a mesh: section: 4 (over z), tensor: 4 (over y, x), dp: 2 (over core).
Axes of the slice: x: 2, y: 2, z: 4, core: 2. Of those that a mesh axis runs over, the one named last changes fastest.
Arguments:
- enc_hidden: bfloat16 [128, 2048], P(('dp', 'tensor'), 'section'), parts along dimension 0, may hold values from -70 to 70
- mlp_gain: float32 [2048], P('section'), may hold values from 0.25 to 1.75
- final_gain: float32 [2048], P('section'), may hold values from 0.25 to 1.75
- w_gate: bfloat16 [2048, 8192], P('section', 'tensor'), may hold values from -0.125 to 0.125
- w_up: bfloat16 [2048, 8192], P('section', 'tensor'), may hold values from -0.125 to 0.125
- w_down: bfloat16 [8192, 2048], P('tensor', 'section'), may hold values from -0.0625 to 0.0625
- key_weight: bfloat16 [4, 2048, 4096], P('section', None, 'tensor'), may hold values from -0.125 to 0.125
- value_weight: bfloat16 [4, 2048, 4096], P('section', None, 'tensor'), may hold values from -0.125 to 0.125
- queries: bfloat16 [4, 2048, 4096], P('section', 'dp', 'tensor'), parts along dimension 1, may hold values from -340 to 340
- context_grad: bfloat16 [4, 2048, 4096], P('section', 'dp', 'tensor'), parts along dimension 1, may hold values from -6 to 6
Outputs:
- query_grad: bfloat16 [4, 2048, 4096], P('section', 'dp', 'tensor'), parts along dimension 1
- hidden_grad: float32 [128, 2048], P(('dp', 'tensor'), 'section'), parts along dimension 0
- gate_weight_grad: bfloat16 [4096, 8192], P(('dp', 'section'), 'tensor'), parts along dimension 0
- up_weight_grad: bfloat16 [4096, 8192], P(('dp', 'section'), 'tensor'), parts along dimension 0
- down_weight_grad: bfloat16 [16384, 2048], P(('dp', 'tensor'), 'section'), parts along dimension 0
There are 2 independent parts, one for each index of `dp`. A program takes and returns all parts, laid end to end along the dimension named above; an argument that names none is the same for every part. Nothing has to cross between parts.
All inputs are finite; a program needn't handle non-finite values.
Results may differ from a plain program's by a relative error of at most 0.017.
Values may be sent and summed in bfloat16 or wider, within the bound.
A program may use at most 64 MiB of HBM per device.

v0:
```python
import functools
import jax
import jax.numpy as jnp
from jax import lax
from jax.experimental import pallas as pl
from jax.experimental.pallas import tpu as pltpu
from jax.sharding import PartitionSpec as P

HEAD = 256
EPSILON = 1e-06
LANES = 128
MESH = pl.DeviceIdType.MESH
VMEM_LIMIT = 58 * 1024 * 1024
ROWS = (((0,), (0,)), ((), ()))
COLS = (((1,), (1,)), ((), ()))
F32 = jnp.float32
BF16 = jnp.bfloat16


def enter(sizes):
    barrier = pltpu.get_barrier_semaphore()
    for axis, n in sizes:
        me = lax.axis_index(axis)
        for k in range(1, n):
            pl.semaphore_signal(
                barrier, inc=1, device_id={axis: lax.rem(me + k, n)}, device_id_type=MESH
            )
    pl.semaphore_wait(barrier, sum(n - 1 for _, n in sizes))


def post(axis, n, source, target, send_sem, recv_sem):
    me = lax.axis_index(axis)
    copies = []
    for k in range(1, n):
        peer = lax.rem(me + k, n)
        copy = pltpu.make_async_remote_copy(
            src_ref=source(peer),
            dst_ref=target(k - 1),
            send_sem=send_sem.at[k - 1],
            recv_sem=recv_sem.at[k - 1],
            device_id={axis: peer},
            device_id_type=MESH,
        )
        copy.start()
        copies.append(copy)
    return copies


def gather(axis, n, ref, send_sem, recv_sem):
    me = lax.axis_index(axis)
    return post(axis, n, lambda peer: ref.at[me], lambda k: ref.at[me], send_sem, recv_sem)


def scatter(axis, n, out, into, send_sem, recv_sem):
    return post(axis, n, lambda peer: out.at[peer], lambda k: into.at[k], send_sem, recv_sem)


def finish(*groups):
    for copies in groups:
        for copy in copies:
            copy.wait()


def total(own, into, n):
    acc = own.astype(F32)
    for k in range(n - 1):
        acc = acc + into[k].astype(F32)
    return acc


def attend(keys, values, q, c):
    scale = HEAD ** (-0.5)
    scores = lax.dot_general(keys, q, COLS, preferred_element_type=F32) * scale
    weights = jnp.exp(scores - jnp.max(scores, axis=0, keepdims=True))
    probs = weights / jnp.sum(weights, axis=0, keepdims=True)
    probs_bf = probs.astype(BF16)
    dprob = lax.dot_general(values, c, COLS, preferred_element_type=F32)
    delta = jnp.sum(probs_bf.astype(F32) * dprob, axis=0, keepdims=True)
    dscore = (probs * (dprob - delta) * scale).astype(BF16)
    query_grad = lax.dot_general(dscore, keys, ROWS, preferred_element_type=F32).astype(BF16)
    key_grad = jnp.dot(dscore, q, preferred_element_type=F32).astype(BF16)
    value_grad = jnp.dot(probs_bf, c, preferred_element_type=F32).astype(BF16)
    return query_grad, key_grad, value_grad


def step_kernel(
    S, N, x_ref, mg_ref, fg_ref, wg_hbm, wu_hbm, wd_hbm, wk_hbm, wv_hbm, q_hbm, c_hbm,
    qg_hbm, hg_out, normed_out, hid_out, oall_out, gate_out, up_out,
    wg, wu, wd, wk, wv, q, c, qg,
    xg, sqs, sqr, gus, gur, hid_all, inv_all, ds, dr, feat, sqo, enc, af, eg,
    r6, s6, r6b, pin, oall, s9, r9, aall, s11, r11, pin2,
    load_sem, store_sem, ssem, rsem,
):
    tt, F = x_ref.shape
    T = N * tt
    ts = T // S
    H = wg.shape[1]
    D = F * S
    heads = q.shape[1] // HEAD
    sec = lax.axis_index("section")
    ten = lax.axis_index("tensor")
    loads = [
        pltpu.make_async_copy(src, dst, load_sem.at[i])
        for i, (src, dst) in enumerate((
            (wg_hbm, wg), (wu_hbm, wu), (wd_hbm, wd), (wk_hbm, wk), (wv_hbm, wv),
            (q_hbm, q), (c_hbm, c),
        ))
    ]
    for load in loads[:3]:
        load.start()
    xg[ten] = x_ref[...]
    enter((("section", S), ("tensor", N)))
    finish(post("tensor", N, lambda p: x_ref, lambda k: xg.at[ten], ssem.at[0], rsem.at[0]))
    wide = xg[...].reshape(T, F).astype(F32)
    scaled = (wide * mg_ref[...]).astype(BF16)
    square = jnp.sum(wide * wide, axis=1, keepdims=True)
    sqs[...] = jnp.broadcast_to(square, (T, LANES)).reshape(S, ts, LANES)
    loads[0].wait()
    gus[0] = jnp.dot(scaled, wg[...], preferred_element_type=F32).astype(BF16).reshape(S, ts, H)
    move_q = scatter("section", S, sqs, sqr, ssem.at[3], rsem.at[3])
    move_g = scatter("section", S, gus.at[0], gur.at[0], ssem.at[1], rsem.at[1])
    loads[1].wait()
    gus[1] = jnp.dot(scaled, wu[...], preferred_element_type=F32).astype(BF16).reshape(S, ts, H)
    move_u = scatter("section", S, gus.at[1], gur.at[1], ssem.at[2], rsem.at[2])
    for load in loads[3:]:
        load.start()
    finish(move_q, move_g)
    inv = lax.rsqrt(total(sqs[sec], sqr, S) / D + EPSILON)
    inv_all[sec] = inv
    inv = inv[:, :1]
    gate_pre = total(gus[0, sec], gur.at[0], S) * inv
    sig = jax.nn.sigmoid(gate_pre)
    act = gate_pre * sig
    af[0, sec] = act.astype(BF16)
    slope = sig * (1.0 + gate_pre * (1.0 - sig))
    finish(move_u)
    up_pre = total(gus[1, sec], gur.at[1], S) * inv
    hid_all[sec] = (act * up_pre).astype(BF16)
    move_h = gather("section", S, hid_all, ssem.at[4], rsem.at[4])
    move_i = gather("section", S, inv_all, ssem.at[5], rsem.at[5])
    af[1, sec] = (up_pre * slope).astype(BF16)
    loads[2].wait()
    finish(move_h)
    hid = hid_all[...].reshape(T, H)
    ds[...] = jnp.dot(hid, wd[...], preferred_element_type=F32).astype(BF16).reshape(N, tt, F)
    move_d = scatter("tensor", N, ds, dr, ssem.at[6], rsem.at[6])
    hid_out[...] = hid
    finish(move_i)
    inv_tok = inv_all[...].reshape(T, LANES)
    normed_out[...] = (wide * inv_tok[:, :1] * mg_ref[...]).astype(BF16)
    finish(move_d)
    outer = x_ref[...].astype(F32) + total(ds[ten], dr, N)
    feat[sec] = (outer * fg_ref[...]).astype(BF16)
    sqo[sec] = jnp.broadcast_to(jnp.sum(outer * outer, axis=1, keepdims=True), (tt, LANES))
    move_s = gather("section", S, sqo, ssem.at[8], rsem.at[8])
    move_f = gather("section", S, feat, ssem.at[7], rsem.at[7])
    finish(move_s, move_f)
    move_act = gather("section", S, af.at[0], ssem.at[10], rsem.at[10])
    move_fac = gather("section", S, af.at[1], ssem.at[11], rsem.at[11])
    inv_o = lax.rsqrt(jnp.sum(sqo[...], axis=0) / D + EPSILON)
    enc[ten] = (feat[...].astype(F32) * inv_o[None, :, :1]).astype(BF16)
    inv_o = inv_o[:, :1]
    move_e = gather("tensor", N, enc, ssem.at[9], rsem.at[9])
    for load in loads[3:]:
        load.wait()
    finish(move_e)

    width = heads * HEAD
    keys = jnp.zeros((T, width), F32)
    values = jnp.zeros((T, width), F32)
    for s in range(S):
        block = enc[:, s].reshape(T, F)
        keys += jnp.dot(block, wk[s * F : (s + 1) * F, :], preferred_element_type=F32)
        values += jnp.dot(block, wv[s * F : (s + 1) * F, :], preferred_element_type=F32)
    keys = keys.astype(BF16)
    values = values.astype(BF16)
    key_grads, value_grads, stores = [], [], []
    for h in range(heads):
        cols = slice(h * HEAD, (h + 1) * HEAD)
        query_grad, key_grad, value_grad = attend(
            keys[:, cols], values[:, cols], q[:, cols], c[:, cols]
        )
        qg[h] = query_grad
        store = pltpu.make_async_copy(qg.at[h], qg_hbm.at[:, cols], store_sem.at[h])
        store.start()
        stores.append(store)
        key_grads.append(key_grad)
        value_grads.append(value_grad)
    key_grad = jnp.concatenate(key_grads, axis=1)
    value_grad = jnp.concatenate(value_grads, axis=1)
    for s in range(S):
        rows = slice(s * F, (s + 1) * F)
        part = lax.dot_general(key_grad, wk[rows, :], COLS, preferred_element_type=F32)
        part += lax.dot_general(value_grad, wv[rows, :], COLS, preferred_element_type=F32)
        eg[:, s] = part.astype(BF16).reshape(N, tt, F)

    finish(scatter("tensor", N, eg, r6, ssem.at[12], rsem.at[12]))
    s6[...] = total(eg[ten], r6, N).astype(BF16)
    finish(scatter("section", S, s6, r6b, ssem.at[13], rsem.at[13]))
    scaled_out = fg_ref[...] * total(s6[sec], r6b, S)
    pin[sec] = jnp.broadcast_to(
        jnp.sum(scaled_out * outer, axis=1, keepdims=True), (tt, LANES)
    )
    finish(gather("section", S, pin, ssem.at[14], rsem.at[14]))
    inner = jnp.sum(pin[...], axis=0)[:, :1] / D
    outer_grad = inv_o * scaled_out - outer * (inv_o * inv_o * inv_o * inner)
    oall[ten] = outer_grad.astype(BF16)
    finish(gather("tensor", N, oall, ssem.at[15], rsem.at[15]))
    grads = oall[...].reshape(T, F)
    half = H // 2
    moves = []
    for i in range(2):
        s9[i] = (
            lax.dot_general(
                grads, wd[i * half : (i + 1) * half, :], COLS, preferred_element_type=F32
            )
            .astype(BF16)
            .reshape(S, ts, half)
        )
        moves.append(scatter("section", S, s9.at[i], r9.at[i], ssem.at[16 + i], rsem.at[16 + i]))
    oall_out[...] = grads
    finish(move_act, move_fac)
    gathers = []
    for i in range(2):
        finish(moves[i])
        aall[i, sec] = total(s9[i, sec], r9.at[i], S).astype(BF16)
        gathers.append(gather("section", S, aall.at[i], ssem.at[18 + i], rsem.at[18 + i]))
    parts = None
    for i in range(2):
        cols = slice(i * half, (i + 1) * half)
        finish(gathers[i])
        act_grad = aall[i].reshape(T, half).astype(F32)
        up_grad = (act_grad * af[0, :, :, cols].reshape(T, half).astype(F32)).astype(BF16)
        gate_grad = (act_grad * af[1, :, :, cols].reshape(T, half).astype(F32)).astype(BF16)
        up_out[:, cols] = up_grad
        gate_out[:, cols] = gate_grad
        part = lax.dot_general(gate_grad, wg[:, cols], COLS, preferred_element_type=F32)
        part += lax.dot_general(up_grad, wu[:, cols], COLS, preferred_element_type=F32)
        parts = part if parts is None else parts + part
    s11[...] = parts.astype(BF16).reshape(N, tt, F)
    finish(scatter("tensor", N, s11, r11, ssem.at[20], rsem.at[20]))
    hidden = x_ref[...].astype(F32)
    scaled_in = mg_ref[...] * total(s11[ten], r11, N)
    pin2[sec] = jnp.broadcast_to(
        jnp.sum(scaled_in * hidden, axis=1, keepdims=True), (tt, LANES)
    )
    finish(gather("section", S, pin2, ssem.at[21], rsem.at[21]))
    inner_in = jnp.sum(pin2[...], axis=0)[:, :1] / D
    inv_flat = inv_all.reshape(T, LANES)
    inv_in = inv_flat[pl.ds(pl.multiple_of(ten * tt, tt), tt), :][:, :1]
    hg_out[...] = (
        outer_grad + inv_in * scaled_in - hidden * (inv_in * inv_in * inv_in * inner_in)
    )
    for store in stores:
        store.wait()


def on_device(
    S, N, enc_hidden, mlp_gain, final_gain, w_gate, w_up, w_down, key_weight, value_weight,
    queries, context_grad,
):
    tt, F = enc_hidden.shape
    T = N * tt
    ts = T // S
    H = w_gate.shape[1]
    peers = max(S, N) - 1
    vmem = pl.BlockSpec(memory_space=pltpu.VMEM)
    hbm = pl.BlockSpec(memory_space=pl.ANY)
    shape = jax.ShapeDtypeStruct
    dma = pltpu.SemaphoreType.DMA
    wk, wv, q, c = key_weight[0], value_weight[0], queries[0], context_grad[0]
    large = (w_gate, w_up, w_down, wk, wv, q, c)
    rows = q.shape[0]
    heads = q.shape[1] // HEAD
    scratch = [pltpu.VMEM(w.shape, BF16) for w in large]
    scratch += [
        pltpu.VMEM((heads, rows, HEAD), BF16),
        pltpu.VMEM((N, tt, F), BF16),
        pltpu.VMEM((S, ts, LANES), F32),
        pltpu.VMEM((S - 1, ts, LANES), F32),
        pltpu.VMEM((2, S, ts, H), BF16),
        pltpu.VMEM((2, S - 1, ts, H), BF16),
        pltpu.VMEM((S, ts, H), BF16),
        pltpu.VMEM((S, ts, LANES), F32),
        pltpu.VMEM((N, tt, F), BF16),
        pltpu.VMEM((N - 1, tt, F), BF16),
        pltpu.VMEM((S, tt, F), BF16),
        pltpu.VMEM((S, tt, LANES), F32),
        pltpu.VMEM((N, S, tt, F), BF16),
        pltpu.VMEM((2, S, ts, H), BF16),
        pltpu.VMEM((N, S, tt, F), BF16),
        pltpu.VMEM((N - 1, S, tt, F), BF16),
        pltpu.VMEM((S, tt, F), BF16),
        pltpu.VMEM((S - 1, tt, F), BF16),
        pltpu.VMEM((S, tt, LANES), F32),
        pltpu.VMEM((N, tt, F), BF16),
        pltpu.VMEM((2, S, ts, H // 2), BF16),
        pltpu.VMEM((2, S - 1, ts, H // 2), BF16),
        pltpu.VMEM((2, S, ts, H // 2), BF16),
        pltpu.VMEM((N, tt, F), BF16),
        pltpu.VMEM((N - 1, tt, F), BF16),
        pltpu.VMEM((S, tt, LANES), F32),
        dma((7,)), dma((heads,)), dma((22, peers)), dma((22, peers)),
    ]
    query_grad, hidden_grad, normed, hid, outer_all, gate_all, up_all = pl.pallas_call(
        functools.partial(step_kernel, S, N),
        out_shape=[
            shape(q.shape, BF16), shape((tt, F), F32), shape((T, F), BF16),
            shape((T, H), BF16), shape((T, F), BF16), shape((T, H), BF16), shape((T, H), BF16),
        ],
        in_specs=[vmem] * 3 + [hbm] * 7,
        out_specs=[hbm] + [vmem] * 6,
        scratch_shapes=scratch,
        compiler_params=pltpu.CompilerParams(
            collective_id=0, has_side_effects=True, vmem_limit_bytes=VMEM_LIMIT
        ),
    )(enc_hidden, mlp_gain[None, :], final_gain[None, :], *large)

    outer_product = lambda a, b: lax.dot_general(
        a, b, ROWS, preferred_element_type=F32
    ).astype(BF16)
    return (
        query_grad[None, :, :],
        hidden_grad,
        outer_product(normed, gate_all),
        outer_product(normed, up_all),
        outer_product(hid, outer_all),
    )


def solution(mesh):
    in_specs = (
        P(("dp", "tensor"), "section"),
        P("section"),
        P("section"),
        P("section", "tensor"),
        P("section", "tensor"),
        P("tensor", "section"),
        P("section", None, "tensor"),
        P("section", None, "tensor"),
        P("section", "dp", "tensor"),
        P("section", "dp", "tensor"),
    )
    out_specs = (
        P("section", "dp", "tensor"),
        P(("dp", "tensor"), "section"),
        P(("dp", "section"), "tensor"),
        P(("dp", "section"), "tensor"),
        P(("dp", "tensor"), "section"),
    )
    body = functools.partial(on_device, mesh.shape["section"], mesh.shape["tensor"])
    return jax.shard_map(
        body, mesh=mesh, in_specs=in_specs, out_specs=out_specs, check_vma=False
    )
```

profile of v0, /device:TPU:0, one launch (start us, length us, event | category | flops | bytes accessed | tf_op | source)
XLA Modules:
  0.0 94.6 jit_solution(2543089153661333619)
XLA Ops:
  0.6 84.8 %shard_map.137 = (bf16[1024,1024]{1,0:T(8,128)(2,1)}, f32[16,512]{1,0:T(8,128)}, bf16[64,512]{1,0:T(8,128)(2,1)}, bf16[64,2048]{1,0:T(8,128)(2,1)}, bf16[64,512]...) custom-call(bf16[16,512]{1,0:T(8,128)(2,1)} %x_ref.1, f32[1,512]{1,0:T(1,128)} %bitcast.18, ...), custom_call_target="tpu_custom_call" | custom-call | tf_op jit(solution)/shard_map/pallas_call | solution.py:305
  85.4 0.0 copy-start.2
  85.4 0.0 copy-start.3
  85.5 0.0 copy-start.1
  85.5 0.0 copy-start.4
  85.5 3.1 %convolution_convert_fusion.2 = bf16[512,2048]{1,0:T(8,128)(2,1)} fusion(bf16[64,512]{1,0:T(8,128)(2,1)} %get-tuple-element.14, bf16[64,2048]{1,0:T(8,128)(2,1)} %get-tuple-element.15), kind=kOutput, calls=%fused_computation.2 | convolution fusion | flops 135266304 | bytes 2424832 | tf_op jit(solution)/shard_map/dot_general | solution.py:319
  88.6 0.0 copy-done.2
  88.6 0.0 copy-done.3
  88.6 0.0 copy-start
  88.6 2.0 %convolution_convert_fusion.1 = bf16[512,2048]{1,0:T(8,128)(2,1)} fusion(bf16[64,512]{1,0:T(8,128)(2,1)S(1)} %copy-done.3, bf16[64,2048]{1,0:T(8,128)(2,1)S(1)} %copy-done.2), kind=kOutput, calls=%fused_computation.1 | convolution fusion | flops 135266304 | bytes 2424832 | tf_op jit(solution)/shard_map/dot_general | solution.py:319
  90.6 0.0 copy-done.1
  90.6 0.0 copy-done.4
  90.6 2.1 %convolution_convert_fusion = bf16[2048,512]{1,0:T(8,128)(2,1)} fusion(bf16[64,2048]{1,0:T(8,128)(2,1)S(1)} %copy-done.1, bf16[64,512]{1,0:T(8,128)(2,1)S(1)} %copy-done.4), kind=kOutput, calls=%fused_computation | convolution fusion | flops 135266304 | bytes 2424832 | tf_op jit(solution)/shard_map/dot_general | solution.py:319
  92.7 0.0 copy-done
  92.7 0.0 copy-start.5
  92.7 1.3 %copy.17 = bf16[1,1024,1024]{2,1,0:T(8,128)(2,1)} copy(bf16[1,1024,1024]{2,1,0:T(8,128)(2,1)S(1)} %bitcast.17) | data formatting | bytes 4194304
  94.0 0.0 copy-done.5
  94.0 0.6 copy.18
Async XLA Ops:
  85.4 3.1 %copy-start.2 = (bf16[64,2048]{1,0:T(8,128)(2,1)S(1)}, bf16[64,2048]{1,0:T(8,128)(2,1)}, u32[]{:S(2)}) copy-start(bf16[64,2048]{1,0:T(8,128)(2,1)} %get-tuple-element.16) | copy-start | bytes 786436
  85.4 3.1 %copy-start.3 = (bf16[64,512]{1,0:T(8,128)(2,1)S(1)}, bf16[64,512]{1,0:T(8,128)(2,1)}, u32[]{:S(2)}) copy-start(bf16[64,512]{1,0:T(8,128)(2,1)} %get-tuple-element.14) | copy-start | bytes 196612
  85.5 5.2 %copy-start.1 = (bf16[64,2048]{1,0:T(8,128)(2,1)S(1)}, bf16[64,2048]{1,0:T(8,128)(2,1)}, u32[]{:S(2)}) copy-start(bf16[64,2048]{1,0:T(8,128)(2,1)} %get-tuple-element.17) | copy-start | bytes 786436
  85.5 5.2 %copy-start.4 = (bf16[64,512]{1,0:T(8,128)(2,1)S(1)}, bf16[64,512]{1,0:T(8,128)(2,1)}, u32[]{:S(2)}) copy-start(bf16[64,512]{1,0:T(8,128)(2,1)} %get-tuple-element.18) | copy-start | bytes 196612
  88.6 4.1 %copy-start = (bf16[1024,1024]{1,0:T(8,128)(2,1)S(1)}, bf16[1024,1024]{1,0:T(8,128)(2,1)}, u32[]{:S(2)}) copy-start(bf16[1024,1024]{1,0:T(8,128)(2,1)} %get-tuple-element.12) | copy-start | bytes 6291460
  92.7 1.3 %copy-start.5 = (f32[16,512]{1,0:T(8,128)S(1)}, f32[16,512]{1,0:T(8,128)}, u32[]{:S(2)}) copy-start(f32[16,512]{1,0:T(8,128)} %get-tuple-element.25) | copy-start | bytes 98308
where the time goes:
time: 94.9 us; the launch traced here: 94.6 us
  Pallas kernels  84.8 us (89%)
  matrix products  7.19 us (8%)
  local copies, waits for them, and re-layouts  1.96 us (2%)
    pallas_call x1, Pallas kernels, on_device(): pl.pallas_call(functools.partial(step_kernel, S, N), out_shape=[shape(q.s...  84.8 us
    dot_general x3, matrix products, on_device(): lax.dot_general(a, b, ROWS, preferred_element_type=F32).astype(BF16)  7.19 us
    unnamed x14, local copies, waits for them, and re-layouts  1.96 us

commit v1 on v0

--- a/solution.py
+++ b/solution.py
@@ -1,3 +1,4 @@
+import contextlib
 import functools
 import jax
 import jax.numpy as jnp
@@ -11,10 +12,16 @@
 LANES = 128
 MESH = pl.DeviceIdType.MESH
 VMEM_LIMIT = 58 * 1024 * 1024
+CHAIN_VMEM_LIMIT = 54 * 1024 * 1024
+WRITE_VMEM_LIMIT = 4 * 1024 * 1024
 ROWS = (((0,), (0,)), ((), ()))
 COLS = (((1,), (1,)), ((), ()))
 F32 = jnp.float32
 BF16 = jnp.bfloat16
+
+
+def mark(name):
+    return contextlib.nullcontext()
 
 
 def enter(sizes):
@@ -255,7 +262,7 @@
         store.wait()
 
 
-def on_device(
+def general(
     S, N, enc_hidden, mlp_gain, final_gain, w_gate, w_up, w_down, key_weight, value_weight,
     queries, context_grad,
 ):
@@ -328,6 +335,495 @@
     )
 
 
+def far_first(n):
+    return sorted(range(1, n), key=lambda k: abs(2 * k - n))
+
+
+def near_first(n):
+    return far_first(n)[::-1]
+
+
+def lane_of_row(rows, offset):
+    row = lax.broadcasted_iota(jnp.int32, (rows, LANES), 0) + offset
+    return (row == lax.broadcasted_iota(jnp.int32, (rows, LANES), 1)).astype(F32)
+
+
+def to_row(column, offset):
+    return jnp.sum(column * lane_of_row(column.shape[0], offset), axis=0, keepdims=True)
+
+
+def to_column(row, rows, offset):
+    return jnp.sum(row * lane_of_row(rows, offset), axis=1, keepdims=True)
+
+
+def exchange(axis, n, k, source, target, send_sem, recv_sem):
+    peer = lax.rem(lax.axis_index(axis) + k, n)
+    copy = pltpu.make_async_remote_copy(
+        src_ref=source(peer),
+        dst_ref=target,
+        send_sem=send_sem.at[k - 1],
+        recv_sem=recv_sem.at[k - 1],
+        device_id={axis: peer},
+        device_id_type=MESH,
+    )
+    copy.start()
+    return copy
+
+
+def everyone(S, N, sections, source, target, send_sem, recv_sem):
+    sec = lax.axis_index("section")
+    ten = lax.axis_index("tensor")
+    copies = {}
+    for k in sections:
+        for j in range(N):
+            if k == 0 and j == 0:
+                continue
+            s = lax.rem(sec + k, S)
+            n = lax.rem(ten + j, N)
+            copy = pltpu.make_async_remote_copy(
+                src_ref=source(s, n),
+                dst_ref=target,
+                send_sem=send_sem.at[k * N + j],
+                recv_sem=recv_sem.at[k * N + j],
+                device_id={"section": s, "tensor": n},
+                device_id_type=MESH,
+            )
+            copy.start()
+            copies[k, j] = copy
+    return copies
+
+
+def product(a, b):
+    return lax.dot_general(a, b, ROWS, preferred_element_type=F32).astype(BF16)
+
+
+def chain_kernel(
+    S, N, x_hbm, mg_hbm, fg_hbm, wg_hbm, wu_hbm, wd_hbm, wk_hbm, wv_hbm, q_hbm, c_hbm,
+    hg_out, qg_out, gw_out, uw_out, dw_out,
+    mg, fg, wg, wu, wd, wk, wv, q, c,
+    xg, sqr, gus, gur, hid, af, comb, ds, dsb, dr, encb, sso, egb, er, ror, oall,
+    s9, r9, aall, rir, gate, up, s11, s11b, r11, rit, rits, dsc,
+    load_sem, ssem, rsem, fsem, sall, rall,
+):
+    tt, F = x_hbm.shape
+    T = N * tt
+    H = wg.shape[1]
+    Hs = H // S
+    D = F * S
+    heads = q.shape[1] // HEAD
+    width = heads * HEAD
+    sec = lax.axis_index("section")
+    ten = lax.axis_index("tensor")
+    sent = []
+
+    def units(p):
+        return pl.ds(pl.multiple_of(p * Hs, LANES), Hs)
+
+    def source_of(k):
+        return lax.rem(sec + S - k, S)
+
+    def share_factor(i, half):
+        part = af.at[i, sec, pl.ds(half * (T // 2), T // 2)]
+        lane = 2 * i + half
+        return [
+            exchange("section", S, k, lambda p: part, part, fsem.at[0, lane], fsem.at[1, lane])
+            for k in far_first(S)
+        ]
+
+    barrier = pltpu.get_barrier_semaphore()
+    for axis, n in (("section", S), ("tensor", N)):
+        me = lax.axis_index(axis)
+        for k in range(1, n):
+            pl.semaphore_signal(
+                barrier, inc=1, device_id={axis: lax.rem(me + k, n)}, device_id_type=MESH
+            )
+    for k in range(1, S):
+        for j in range(1, N):
+            pl.semaphore_signal(
+                barrier,
+                inc=1,
+                device_id={"section": lax.rem(sec + k, S), "tensor": lax.rem(ten + j, N)},
+                device_id_type=MESH,
+            )
+    loads = [
+        pltpu.make_async_copy(src, dst, load_sem.at[i])
+        for i, (src, dst) in enumerate((
+            (x_hbm, xg.at[ten]), (mg_hbm, mg), (fg_hbm, fg),
+            (wg_hbm, wg), (wu_hbm, wu), (wd_hbm, wd), (wk_hbm, wk), (wv_hbm, wv),
+            (q_hbm, q), (c_hbm, c),
+        ))
+    ]
+    for load in loads[:6]:
+        load.start()
+    loads[0].wait()
+    with mark("enter"):
+        pl.semaphore_wait(barrier, S * N - 1)
+    moves = [
+        exchange("tensor", N, k, lambda p: xg.at[ten], xg.at[ten], ssem.at[0], rsem.at[0])
+        for k in far_first(N)
+    ]
+    for load in loads[1:5]:
+        load.wait()
+    with mark("x"):
+        for move in moves:
+            move.wait_recv()
+    sent += moves
+
+    wide = xg[...].reshape(T, F).astype(F32)
+    scaled = (wide * mg[...]).astype(BF16)
+    square = jnp.sum(wide * wide, axis=1, keepdims=True)
+    sqr[sec] = to_row(square, 0)
+    move_q = [
+        exchange("section", S, k, lambda p: sqr.at[sec], sqr.at[sec], ssem.at[1], rsem.at[1])
+        for k in far_first(S)
+    ]
+    move_g, move_u = {}, {}
+    for k in far_first(S):
+        p = lax.rem(sec + k, S)
+        gus[0, p] = jnp.dot(scaled, wg[:, units(p)], preferred_element_type=F32).astype(BF16)
+        move_g[k] = exchange(
+            "section", S, k, lambda p: gus.at[0, p], gur.at[0, k - 1], ssem.at[2], rsem.at[2]
+        )
+        gus[1, p] = jnp.dot(scaled, wu[:, units(p)], preferred_element_type=F32).astype(BF16)
+        move_u[k] = exchange(
+            "section", S, k, lambda p: gus.at[1, p], gur.at[1, k - 1], ssem.at[3], rsem.at[3]
+        )
+    for load in loads[6:]:
+        load.start()
+    gate_pre = jnp.dot(scaled, wg[:, units(sec)], preferred_element_type=F32)
+    up_pre = jnp.dot(scaled, wu[:, units(sec)], preferred_element_type=F32)
+    with mark("sq"):
+        for move in move_q:
+            move.wait_recv()
+    sent += move_q
+    inv = lax.rsqrt(to_column(jnp.sum(sqr[...], axis=0), T, 0) / D + EPSILON)
+    normed = (wide * inv * mg[...]).astype(BF16)
+    loads[5].wait()
+    for k in near_first(S):
+        with mark(f"gu{k}"):
+            move_g[k].wait_recv()
+            move_u[k].wait_recv()
+        gate_pre = gate_pre + gur[0, k - 1].astype(F32)
+        up_pre = up_pre + gur[1, k - 1].astype(F32)
+        sent += [move_g[k], move_u[k]]
+    gate_pre = gate_pre * inv
+    up_pre = up_pre * inv
+    sig = jax.nn.sigmoid(gate_pre)
+    act = gate_pre * sig
+    hid[sec] = (act * up_pre).astype(BF16)
+    move_h = {
+        k: exchange("section", S, k, lambda p: hid.at[sec], hid.at[sec], ssem.at[4], rsem.at[4])
+        for k in far_first(S)
+    }
+    factor = up_pre * (sig * (1.0 + gate_pre * (1.0 - sig)))
+    af[0, sec] = act.astype(BF16)
+    af[1, sec] = factor.astype(BF16)
+    comb[...] = act * up_pre + factor * gate_pre
+    down = jnp.dot(hid[sec], wd[units(sec), :], preferred_element_type=F32)
+    for k in near_first(S):
+        with mark(f"hid{k}"):
+            move_h[k].wait_recv()
+        p = source_of(k)
+        down = down + jnp.dot(hid[p], wd[units(p), :], preferred_element_type=F32)
+        sent.append(move_h[k])
+    ds[...] = down.reshape(N, tt, F)
+    dsb[...] = down.astype(BF16).reshape(N, tt, F)
+    moves = [
+        exchange("tensor", N, k, lambda p: dsb.at[p], dr.at[k - 1], ssem.at[5], rsem.at[5])
+        for k in far_first(N)
+    ]
+    move_a = share_factor(0, 0)
+    with mark("ds"):
+        for move in moves:
+            move.wait_recv()
+    sent += moves
+    outer = xg[ten].astype(F32) + total(ds[ten], dr, N)
+    sso[sec, ten] = to_row(jnp.sum(outer * outer, axis=1, keepdims=True), ten * tt)
+    encb[sec, ten] = (outer * fg[...]).astype(BF16)
+    order = [0] + near_first(S)
+    move_s = everyone(
+        S, N, order, lambda s, n: sso.at[sec, ten], sso.at[sec, ten], sall.at[1], rall.at[1]
+    )
+    move_e = {}
+
+    def send_block(block, axis, peer, k, j):
+        move_e[k, j] = pltpu.make_async_remote_copy(
+            src_ref=block,
+            dst_ref=block,
+            send_sem=sall.at[0, k * N + j],
+            recv_sem=rall.at[0, k * N + j],
+            device_id={axis: peer},
+            device_id_type=MESH,
+        )
+        move_e[k, j].start()
+
+    for k in far_first(S):
+        send_block(encb.at[sec, ten], "section", lax.rem(sec + k, S), k, 0)
+    for j in far_first(N):
+        send_block(encb.at[sec, ten], "tensor", lax.rem(ten + j, N), 0, j)
+    move_a += share_factor(0, 1) + share_factor(1, 0) + share_factor(1, 1)
+    for k in order[1:]:
+        with mark(f"pass{k}"):
+            move_e[k, 0].wait_recv()
+        for j in far_first(N):
+            send_block(encb.at[source_of(k), ten], "tensor", lax.rem(ten + j, N), k, j)
+    sent += list(move_e.values()) + list(move_s.values())
+    for load in loads[6:]:
+        load.wait()
+    keys = values = None
+    for k in order:
+        with mark(f"enc{k}"):
+            for j in range(1, N):
+                move_e[k, j].wait_recv()
+        p = source_of(k)
+        block = encb[p].reshape(T, F)
+        rows = pl.ds(pl.multiple_of(p * F, F), F)
+        key_part = jnp.dot(block, wk[rows, :], preferred_element_type=F32)
+        value_part = jnp.dot(block, wv[rows, :], preferred_element_type=F32)
+        keys = key_part if keys is None else keys + key_part
+        values = value_part if values is None else values + value_part
+    with mark("sso"):
+        for move in move_s.values():
+            move.wait_recv()
+    squares = jnp.sum(sso[...].reshape(S * N, 1, LANES), axis=0)
+    inv_all = lax.rsqrt(to_column(squares, T, 0) / D + EPSILON)
+    inv_o = lax.rsqrt(to_column(squares, tt, ten * tt) / D + EPSILON)
+    keys = (keys * inv_all).astype(BF16)
+    values = (values * inv_all).astype(BF16)
+    scale = HEAD ** (-0.5)
+    key_grads, value_grads = [], []
+    inner = None
+    for h in range(heads):
+        cols = slice(h * HEAD, (h + 1) * HEAD)
+        scores = lax.dot_general(keys[:, cols], q[:, cols], COLS, preferred_element_type=F32)
+        scores = scores * scale
+        weights = jnp.exp(scores - jnp.max(scores, axis=0, keepdims=True))
+        probs = weights / jnp.sum(weights, axis=0, keepdims=True)
+        probs_bf = probs.astype(BF16)
+        dprob = lax.dot_general(values[:, cols], c[:, cols], COLS, preferred_element_type=F32)
+        delta = jnp.sum(probs_bf.astype(F32) * dprob, axis=0, keepdims=True)
+        dscore = (probs * (dprob - delta) * scale).astype(BF16)
+        dsc[h] = dscore
+        key_grad = jnp.dot(dscore, q[:, cols], preferred_element_type=F32).astype(BF16)
+        value_grad = jnp.dot(probs_bf, c[:, cols], preferred_element_type=F32).astype(BF16)
+        part = key_grad.astype(F32) * keys[:, cols].astype(F32)
+        part += value_grad.astype(F32) * values[:, cols].astype(F32)
+        inner = part if inner is None else inner + part
+        key_grads.append(key_grad)
+        value_grads.append(value_grad)
+    key_grad = jnp.concatenate(key_grads, axis=1)
+    value_grad = jnp.concatenate(value_grads, axis=1)
+    ror[sec, ten] = to_row(jnp.sum(inner, axis=1, keepdims=True), 0)
+    move_r = everyone(
+        S, N, far_first(S) + [0], lambda s, n: ror.at[sec, ten], ror.at[sec, ten],
+        sall.at[2], rall.at[2],
+    )
+    move_g = {}
+    for k in far_first(S) + [0]:
+        p = lax.rem(sec + k, S)
+        rows = pl.ds(pl.multiple_of(p * F, F), F)
+        part = lax.dot_general(key_grad, wk[rows, :], COLS, preferred_element_type=F32)
+        part += lax.dot_general(value_grad, wv[rows, :], COLS, preferred_element_type=F32)
+        egb[p] = part.astype(BF16).reshape(N, tt, F)
+        move_g.update(everyone(
+            S, N, [k], lambda s, n: egb.at[s, n], er.at[sec, ten], sall.at[3], rall.at[3]
+        ))
+    er[sec, ten] = egb[sec, ten]
+    for h in range(heads):
+        cols = slice(h * HEAD, (h + 1) * HEAD)
+        qg_out[:, cols] = product(dsc[h], keys[:, cols])
+    sent += list(move_g.values()) + list(move_r.values())
+    with mark("eg"):
+        for move in move_r.values():
+            move.wait_recv()
+        for move in move_g.values():
+            move.wait_recv()
+    inner = to_column(jnp.sum(ror[...].reshape(S * N, 1, LANES), axis=0), tt, ten * tt)
+    grad = jnp.sum(er[...].reshape(S * N, tt, F).astype(F32), axis=0)
+    outer_grad = inv_o * (fg[...] * grad) - outer * (inv_o * inv_o * inner / D)
+    oall[ten] = outer_grad.astype(BF16)
+    moves = [
+        exchange("tensor", N, k, lambda p: oall.at[ten], oall.at[ten], ssem.at[8], rsem.at[8])
+        for k in far_first(N)
+    ]
+    with mark("oall"):
+        for move in moves:
+            move.wait_recv()
+    sent += moves
+    grads = oall[...].reshape(T, F)
+    move_9 = {}
+    for k in far_first(S):
+        p = lax.rem(sec + k, S)
+        s9[p] = lax.dot_general(
+            grads, wd[units(p), :], COLS, preferred_element_type=F32
+        ).astype(BF16)
+        move_9[k] = exchange(
+            "section", S, k, lambda p: s9.at[p], r9.at[k - 1], ssem.at[9], rsem.at[9]
+        )
+    act_grad = lax.dot_general(grads, wd[units(sec), :], COLS, preferred_element_type=F32)
+    for s in range(S):
+        dw_out[s * Hs : (s + 1) * Hs, :] = product(hid[s], grads)
+    for k in near_first(S):
+        with mark(f"s9_{k}"):
+            move_9[k].wait_recv()
+        act_grad = act_grad + r9[k - 1].astype(F32)
+        sent.append(move_9[k])
+    aall[sec] = act_grad.astype(BF16)
+    move_g = {
+        k: exchange("section", S, k, lambda p: aall.at[sec], aall.at[sec], ssem.at[10], rsem.at[10])
+        for k in far_first(S)
+    }
+    rir[sec] = to_row(jnp.sum(act_grad * comb[...], axis=1, keepdims=True), 0)
+    move_r = [
+        exchange("section", S, k, lambda p: rir.at[sec], rir.at[sec], ssem.at[11], rsem.at[11])
+        for k in far_first(S)
+    ]
+    with mark("af"):
+        for move in move_a:
+            move.wait_recv()
+    sent += move_a + move_r
+    part = None
+    for k in [0] + near_first(S):
+        p = source_of(k)
+        if k:
+            with mark(f"aall{k}"):
+                move_g[k].wait_recv()
+            sent.append(move_g[k])
+        act_grad = aall[p].astype(F32)
+        up_grad = (act_grad * af[0, p].astype(F32)).astype(BF16)
+        gate_grad = (act_grad * af[1, p].astype(F32)).astype(BF16)
+        up[p] = up_grad
+        gate[p] = gate_grad
+        more = lax.dot_general(gate_grad, wg[:, units(p)], COLS, preferred_element_type=F32)
+        more += lax.dot_general(up_grad, wu[:, units(p)], COLS, preferred_element_type=F32)
+        part = more if part is None else part + more
+    for move in move_r:
+        move.wait_recv()
+    s11[...] = part.reshape(N, tt, F)
+    s11b[...] = part.astype(BF16).reshape(N, tt, F)
+    moves = [
+        exchange("tensor", N, k, lambda p: s11b.at[p], r11.at[k - 1], ssem.at[12], rsem.at[12])
+        for k in far_first(N)
+    ]
+    rits[...] = jnp.sum(rir[...], axis=0)
+    more_moves = [
+        exchange("tensor", N, k, lambda p: rits, rit.at[k - 1], ssem.at[13], rsem.at[13])
+        for k in far_first(N)
+    ]
+    for s in range(S):
+        cols = slice(s * Hs, (s + 1) * Hs)
+        gw_out[:, cols] = product(normed, gate[s])
+        uw_out[:, cols] = product(normed, up[s])
+    with mark("s11"):
+        for move in moves + more_moves:
+            move.wait_recv()
+    sent += moves + more_moves
+    hidden = xg[ten].astype(F32)
+    scaled_in = mg[...] * total(s11[ten], r11, N)
+    inner = to_column(total(rits[...], rit, N), tt, ten * tt)
+    squares = to_column(jnp.sum(sqr[...], axis=0), tt, ten * tt)
+    inv_in = lax.rsqrt(squares / D + EPSILON)
+    hg_out[...] = outer_grad + inv_in * scaled_in - hidden * (inv_in * inv_in * inner / D)
+    with mark("end"):
+        for move in sent:
+            move.wait_send()
+
+
+def write_kernel(*refs):
+    count = len(refs) // 2
+    sem = refs[-1]
+    copies = [
+        pltpu.make_async_copy(refs[i], refs[count + i], sem.at[i]) for i in range(count)
+    ]
+    for copy in copies:
+        copy.start()
+    for copy in copies:
+        copy.wait()
+
+
+def fast(
+    S, N, enc_hidden, mlp_gain, final_gain, w_gate, w_up, w_down, key_weight, value_weight,
+    queries, context_grad,
+):
+    tt, F = enc_hidden.shape
+    T = N * tt
+    H = w_gate.shape[1]
+    Hs = H // S
+    vmem = pl.BlockSpec(memory_space=pltpu.VMEM)
+    hbm = pl.BlockSpec(memory_space=pltpu.HBM)
+    shape = jax.ShapeDtypeStruct
+    dma = pltpu.SemaphoreType.DMA
+    wk, wv, q, c = key_weight[0], value_weight[0], queries[0], context_grad[0]
+    rows, width = q.shape
+    heads = width // HEAD
+    buf = lambda *dims: pltpu.VMEM(dims, BF16)
+    wide = lambda *dims: pltpu.VMEM(dims, F32)
+    scratch = [
+        wide(1, F), wide(1, F), buf(F, H), buf(F, H), buf(H, F), buf(*wk.shape), buf(*wv.shape),
+        buf(rows, width), buf(rows, width),
+        buf(N, tt, F),
+        wide(S, 1, LANES),
+        buf(2, S, T, Hs),
+        buf(2, S - 1, T, Hs),
+        buf(S, T, Hs),
+        buf(2, S, T, Hs),
+        wide(T, Hs),
+        wide(N, tt, F),
+        buf(N, tt, F),
+        buf(N - 1, tt, F),
+        buf(S, N, tt, F),
+        wide(S, N, 1, LANES),
+        buf(S, N, tt, F),
+        buf(S, N, tt, F),
+        wide(S, N, 1, LANES),
+        buf(N, tt, F),
+        buf(S, T, Hs),
+        buf(S - 1, T, Hs),
+        buf(S, T, Hs),
+        wide(S, 1, LANES),
+        buf(S, T, Hs),
+        buf(S, T, Hs),
+        wide(N, tt, F),
+        buf(N, tt, F),
+        buf(N - 1, tt, F),
+        wide(N - 1, 1, LANES),
+        wide(1, LANES),
+        buf(heads, T, rows),
+        dma((10,)), dma((14, max(S, N) - 1)), dma((14, max(S, N) - 1)),
+        dma((2, 4, S - 1)), dma((4, S * N)), dma((4, S * N)),
+    ]
+    results = [
+        ((tt, F), F32), ((rows, width), BF16), ((F, H), BF16), ((F, H), BF16), ((H, F), BF16)
+    ]
+    made = pl.pallas_call(
+        functools.partial(chain_kernel, S, N),
+        out_shape=[pltpu.VMEM(*result) for result in results],
+        in_specs=[hbm] * 10,
+        out_specs=[vmem] * 5,
+        scratch_shapes=scratch,
+        compiler_params=pltpu.CompilerParams(
+            collective_id=0, has_side_effects=True, vmem_limit_bytes=CHAIN_VMEM_LIMIT
+        ),
+    )(enc_hidden, mlp_gain[None, :], final_gain[None, :], w_gate, w_up, w_down, wk, wv, q, c)
+    hidden_grad, query_grad, gate_grad, up_grad, down_grad = pl.pallas_call(
+        write_kernel,
+        out_shape=[shape(*result) for result in results],
+        in_specs=[vmem] * 5,
+        out_specs=[hbm] * 5,
+        scratch_shapes=[dma((5,))],
+        compiler_params=pltpu.CompilerParams(vmem_limit_bytes=WRITE_VMEM_LIMIT),
+    )(*made)
+    return query_grad[None, :, :], hidden_grad, gate_grad, up_grad, down_grad
+
+
+def on_device(S, N, enc_hidden, mlp_gain, final_gain, w_gate, *rest):
+    tt, F = enc_hidden.shape
+    Hs = w_gate.shape[1] // S
+    fits = Hs % LANES == 0 and F % LANES == 0 and tt % 16 == 0 and N * tt <= LANES
+    run = fast if fits else general
+    return run(S, N, enc_hidden, mlp_gain, final_gain, w_gate, *rest)
+
+
 def solution(mesh):
     in_specs = (
         P(("dp", "tensor"), "section"),

time: 94.9 us -> 78.8 us (0.83)
  matrix products: 7.19 us -> 0 us
  Pallas kernels: 84.8 us -> 77.9 us
  local copies, waits for them, and re-layouts: 1.96 us -> 0 us
    dot_general x3 -> x0, matrix products: 7.19 us -> none  [on_device(): lax.dot_general(a, b, ROWS, preferred_element_type=F32).astype(BF16)]
    pallas_call x1 -> x2, Pallas kernels: 84.8 us -> 77.9 us  [the longest x1 74.5 us: fast(): pl.pallas_call(functools.partial(chain_kernel, S, N), out_shape=[pltpu.VM...]
    unnamed x14 -> x0, local copies, waits for them, and re-layouts: 1.96 us -> none
where the time goes in v1:
time: 78.8 us; the launch traced here: 78.6 us
  Pallas kernels  77.9 us (99%)
    pallas_call x1, Pallas kernels, fast(): pl.pallas_call(functools.partial(chain_kernel, S, N), out_shape=[pltpu.VM...  74.5 us
    pallas_call x1, Pallas kernels, fast(): pl.pallas_call(write_kernel, out_shape=[shape(*result) for result in resu...  3.39 us

profile of v1, /device:TPU:0, one launch (start us, length us, event | category | flops | bytes accessed | tf_op | source)
XLA Modules:
  0.0 78.6 jit_solution(1200077519187918283)
XLA Ops:
  0.6 74.5 %shard_map.137 = (f32[16,512]{1,0:T(8,128)S(1)}, bf16[1024,1024]{1,0:T(8,128)(2,1)S(1)}, bf16[512,2048]{1,0:T(8,128)(2,1)S(1)}, bf16[512,2048]{1,0:T(8,128)(2,1)S(1)}, bf16[2048,512]{1,0:T(8,128)(2,1)S(1)}) custom-call(bf16[16,512]{1,0:T(8,128)(2,1)} %x_hbm.1, f32[1,512]{1,0:T(1,128)} %bitcast.11, f32[1,512]{1,0:T(1,128)} %bitcast.12, ...), custom_call_target="tpu_custom_call" | custom-call | tf_op jit(solution)/shard_map/pallas_call | solution.py:798
  75.2 3.4 %shard_map.138 = (f32[16,512]{1,0:T(8,128)}, bf16[1024,1024]{1,0:T(8,128)(2,1)}, bf16[512,2048]{1,0:T(8,128)(2,1)}, bf16[512,2048]{1,0:T(8,128)(2,1)}, bf16[2048,512]{1,0:T(8,128)(2,1)}) custom-call(f32[16,512]{1,0:T(8,128)S(1)} %get-tuple-element.15.refs_0_, bf16[1024,1024]{1,0:T(8,128)(2,1)S(1)} %get-tuple-element.16.refs_1_, ...), custom_call_target="tpu_custom_call" | custom-call | tf_op jit(solution)/shard_map/pallas_call | solution.py:808

commit v2 on v0

--- a/solution.py
+++ b/solution.py
@@ -1,3 +1,4 @@
+import contextlib
 import functools
 import jax
 import jax.numpy as jnp
@@ -11,10 +12,16 @@
 LANES = 128
 MESH = pl.DeviceIdType.MESH
 VMEM_LIMIT = 58 * 1024 * 1024
+CHAIN_VMEM_LIMIT = 54 * 1024 * 1024
+WRITE_VMEM_LIMIT = 4 * 1024 * 1024
 ROWS = (((0,), (0,)), ((), ()))
 COLS = (((1,), (1,)), ((), ()))
 F32 = jnp.float32
 BF16 = jnp.bfloat16
+
+
+def mark(name):
+    return contextlib.nullcontext()
 
 
 def enter(sizes):
@@ -255,7 +262,7 @@
         store.wait()
 
 
-def on_device(
+def general(
     S, N, enc_hidden, mlp_gain, final_gain, w_gate, w_up, w_down, key_weight, value_weight,
     queries, context_grad,
 ):
@@ -328,6 +335,432 @@
     )
 
 
+def lane_of_row(rows, offset):
+    row = lax.broadcasted_iota(jnp.int32, (rows, LANES), 0) + offset
+    return (row == lax.broadcasted_iota(jnp.int32, (rows, LANES), 1)).astype(F32)
+
+
+def to_row(column, offset):
+    return jnp.sum(column * lane_of_row(column.shape[0], offset), axis=0, keepdims=True)
+
+
+def to_column(row, rows, offset):
+    return jnp.sum(row * lane_of_row(rows, offset), axis=1, keepdims=True)
+
+
+def send(source, target, send_sem, recv_sem, **peer):
+    pltpu.make_async_remote_copy(
+        src_ref=source,
+        dst_ref=target,
+        send_sem=send_sem,
+        recv_sem=recv_sem,
+        device_id=peer,
+        device_id_type=MESH,
+    ).start()
+
+
+def arrive(cover, sem):
+    pltpu.make_async_copy(cover, cover, sem).wait()
+
+
+def product(a, b):
+    return lax.dot_general(a, b, ROWS, preferred_element_type=F32).astype(BF16)
+
+
+def chain_kernel(
+    S, N, x_hbm, mg_hbm, fg_hbm, wg_hbm, wu_hbm, wd_hbm, wk_hbm, wv_hbm, q_hbm, c_hbm,
+    hg_out, qg_out, gw_out, uw_out, dw_out,
+    gains, wgu, wd, wkv, qc,
+    xg, sqr, gus, gur, hid, af, comb, ds, dsb, dr, encb, sso, egb, er, ror, oall,
+    s9, r9, aall, rir, gate, up, s11, s11b, r11, rit, dsc,
+    load_sem, ssem, rsem, psem,
+):
+    tt, F = x_hbm.shape
+    T = N * tt
+    H = wd.shape[0]
+    Hs = H // S
+    D = F * S
+    heads = qc.shape[2] // HEAD
+    sec = lax.axis_index("section")
+    ten = lax.axis_index("tensor")
+    turn = 1 - 2 * (sec // ((S + 1) // 2))
+    sent = []
+
+    def section(k):
+        return lax.rem(sec + turn * k + S, S)
+
+    def tensor(k):
+        return lax.rem(ten + k, N)
+
+    low = (1 - turn) // 2
+    rank = low * (S - 1) + turn * sec
+
+    def distant(i):
+        other = S - 1 - i - (i + rank) // (S - 1)
+        return low * (S - 1) + turn * other
+
+    near = range(1, S)
+    far = [distant(i) for i in range(S - 1)]
+    across = range(1, N)
+
+    def units(p):
+        return pl.ds(pl.multiple_of(p * Hs, LANES), Hs)
+
+    def features(p):
+        return pl.ds(pl.multiple_of(p * F, F), F)
+
+    def others(ref):
+        return ref.at[pl.ds(0, ref.shape[0] - 1)]
+
+    def to_tensor(lane, source, target, cover):
+        for k in across:
+            send(source(tensor(k)), target, ssem.at[lane], rsem.at[lane], tensor=tensor(k))
+        sent.append((cover, lane))
+
+    def to_section(lane, source, target, cover, sem=None):
+        for p in far:
+            send(
+                source(p), target, ssem.at[lane], rsem.at[lane] if sem is None else sem, section=p
+            )
+        sent.append((cover, lane))
+
+    def to_everyone(lane, source, target, sections):
+        for p in sections:
+            for j in range(N):
+                if p is not sec or j:
+                    send(
+                        source(p, tensor(j)), target, ssem.at[lane], rsem.at[lane],
+                        section=p, tensor=tensor(j),
+                    )
+
+    barrier = pltpu.get_barrier_semaphore()
+    for k in range(S):
+        for j in range(N):
+            if k or j:
+                pl.semaphore_signal(
+                    barrier,
+                    inc=1,
+                    device_id={"section": section(k), "tensor": tensor(j)},
+                    device_id_type=MESH,
+                )
+    loads = [
+        pltpu.make_async_copy(src, dst, load_sem.at[i])
+        for src, dst, i in (
+            (x_hbm, xg.at[ten], 0), (mg_hbm, gains.at[0], 1), (fg_hbm, gains.at[1], 1),
+            (wg_hbm, wgu.at[0], 2), (wu_hbm, wgu.at[1], 2), (wd_hbm, wd, 3),
+            (wk_hbm, wkv.at[0], 4), (wv_hbm, wkv.at[1], 4),
+            (q_hbm, qc.at[0], 5), (c_hbm, qc.at[1], 5),
+        )
+    ]
+    for load in loads[:6]:
+        load.start()
+    loads[0].wait()
+    with mark("enter"):
+        pl.semaphore_wait(barrier, S * N - 1)
+    to_tensor(0, lambda p: xg.at[ten], xg.at[ten], others(xg))
+    arrive(gains, load_sem.at[1])
+    arrive(wgu, load_sem.at[2])
+    mg, fg = gains.at[0], gains.at[1]
+    wg, wu = wgu.at[0], wgu.at[1]
+    wk, wv = wkv.at[0], wkv.at[1]
+    with mark("x"):
+        arrive(others(xg), rsem.at[0])
+
+    wide = xg[...].reshape(T, F).astype(F32)
+    scaled = (wide * mg[...]).astype(BF16)
+    square = jnp.sum(wide * wide, axis=1, keepdims=True)
+    sqr[sec] = to_row(square, 0)
+    to_section(1, lambda p: sqr.at[sec], sqr.at[sec], others(sqr))
+    for p in far:
+        gus[p, 0] = jnp.dot(scaled, wg[:, units(p)], preferred_element_type=F32).astype(BF16)
+        gus[p, 1] = jnp.dot(scaled, wu[:, units(p)], preferred_element_type=F32).astype(BF16)
+        send(gus.at[p], gur.at[sec], ssem.at[2], rsem.at[2], section=p)
+    sent.append((others(gus), 2))
+    for load in loads[6:]:
+        load.start()
+    gate_pre = jnp.dot(scaled, wg[:, units(sec)], preferred_element_type=F32)
+    up_pre = jnp.dot(scaled, wu[:, units(sec)], preferred_element_type=F32)
+    with mark("sq"):
+        arrive(others(sqr), rsem.at[1])
+    inv = lax.rsqrt(to_column(jnp.sum(sqr[...], axis=0), T, 0) / D + EPSILON)
+    normed = (wide * inv * mg[...]).astype(BF16)
+    loads[5].wait()
+    with mark("gu"):
+        arrive(others(gur), rsem.at[2])
+    for k in near:
+        gate_pre = gate_pre + gur[section(k), 0].astype(F32)
+        up_pre = up_pre + gur[section(k), 1].astype(F32)
+    gate_pre = gate_pre * inv
+    up_pre = up_pre * inv
+    sig = jax.nn.sigmoid(gate_pre)
+    act = gate_pre * sig
+    hid[sec] = (act * up_pre).astype(BF16)
+    to_section(3, lambda p: hid.at[sec], hid.at[sec], others(hid), psem.at[0, sec])
+    factor = up_pre * (sig * (1.0 + gate_pre * (1.0 - sig)))
+    piece = T // 2
+    af[sec, 0] = act[:piece].astype(BF16)
+    af[sec, 1] = act[piece:].astype(BF16)
+    af[sec, 2] = factor[:piece].astype(BF16)
+    af[sec, 3] = factor[piece:].astype(BF16)
+    comb[...] = act * up_pre + factor * gate_pre
+    down = jnp.dot(hid[sec], wd[units(sec), :], preferred_element_type=F32)
+    for k in near:
+        p = section(k)
+        with mark(f"hid{k}"):
+            arrive(hid.at[p], psem.at[0, p])
+        down = down + jnp.dot(hid[p], wd[units(p), :], preferred_element_type=F32)
+    ds[...] = down.reshape(N, tt, F)
+    dsb[...] = down.astype(BF16).reshape(N, tt, F)
+    to_tensor(4, lambda p: dsb.at[p], dr.at[ten], others(dsb))
+    early = lambda p: af.at[p, pl.ds(0, 1)]
+    late = lambda p: af.at[p, pl.ds(1, 3)]
+    to_section(5, lambda p: early(sec), early(sec), af.at[pl.ds(0, S - 1), pl.ds(0, 1)])
+    with mark("ds"):
+        arrive(others(dr), rsem.at[4])
+    outer = xg[ten].astype(F32) + ds[ten]
+    for k in across:
+        outer = outer + dr[tensor(k)].astype(F32)
+    me = sec * N + ten
+    sso[me] = to_row(jnp.sum(outer * outer, axis=1, keepdims=True), ten * tt)
+    encb[me] = (outer * fg[...]).astype(BF16)
+    to_everyone(6, lambda s, n: sso.at[me], sso.at[me], [*far, sec])
+    sent.append((others(sso), 6))
+    for p in far:
+        send(encb.at[me], encb.at[me], ssem.at[7], psem.at[1, sec], section=p)
+    for k in across:
+        send(encb.at[me], encb.at[me], ssem.at[7], psem.at[2, sec], tensor=tensor(k))
+    for k in near:
+        block = section(k) * N + ten
+        with mark(f"pass{k}"):
+            arrive(encb.at[block], psem.at[1, section(k)])
+        for j in across:
+            send(
+                encb.at[block], encb.at[block], ssem.at[7], psem.at[2, section(k)],
+                tensor=tensor(j),
+            )
+    sent.append((others(encb), 7))
+    to_section(8, lambda p: late(sec), late(sec), af.at[pl.ds(0, S - 1), pl.ds(1, 3)])
+    arrive(wkv, load_sem.at[4])
+    arrive(qc, load_sem.at[5])
+    keys = values = None
+    for k in range(S):
+        p = section(k)
+        with mark(f"enc{k}"):
+            arrive(encb.at[pl.ds(0, N - 1)], psem.at[2, p])
+        block = encb[pl.ds(p * N, N)].reshape(T, F)
+        key_part = jnp.dot(block, wk[features(p), :], preferred_element_type=F32)
+        value_part = jnp.dot(block, wv[features(p), :], preferred_element_type=F32)
+        keys = key_part if keys is None else keys + key_part
+        values = value_part if values is None else values + value_part
+    with mark("sso"):
+        arrive(others(sso), rsem.at[6])
+    squares = jnp.sum(sso[...], axis=0)
+    inv_all = lax.rsqrt(to_column(squares, T, 0) / D + EPSILON)
+    inv_o = lax.rsqrt(to_column(squares, tt, ten * tt) / D + EPSILON)
+    keys = (keys * inv_all).astype(BF16)
+    values = (values * inv_all).astype(BF16)
+    scale = HEAD ** (-0.5)
+    key_grads, value_grads = [], []
+    inner = None
+    for h in range(heads):
+        cols = slice(h * HEAD, (h + 1) * HEAD)
+        q, c = qc[0, :, cols], qc[1, :, cols]
+        scores = lax.dot_general(keys[:, cols], q, COLS, preferred_element_type=F32) * scale
+        weights = jnp.exp(scores - jnp.max(scores, axis=0, keepdims=True))
+        probs = weights / jnp.sum(weights, axis=0, keepdims=True)
+        probs_bf = probs.astype(BF16)
+        dprob = lax.dot_general(values[:, cols], c, COLS, preferred_element_type=F32)
+        delta = jnp.sum(probs_bf.astype(F32) * dprob, axis=0, keepdims=True)
+        dscore = (probs * (dprob - delta) * scale).astype(BF16)
+        dsc[h] = dscore
+        key_grad = jnp.dot(dscore, q, preferred_element_type=F32).astype(BF16)
+        value_grad = jnp.dot(probs_bf, c, preferred_element_type=F32).astype(BF16)
+        part = key_grad.astype(F32) * keys[:, cols].astype(F32)
+        part += value_grad.astype(F32) * values[:, cols].astype(F32)
+        inner = part if inner is None else inner + part
+        key_grads.append(key_grad)
+        value_grads.append(value_grad)
+    key_grad = jnp.concatenate(key_grads, axis=1)
+    value_grad = jnp.concatenate(value_grads, axis=1)
+    ror[me] = to_row(jnp.sum(inner, axis=1, keepdims=True), 0)
+    to_everyone(9, lambda s, n: ror.at[me], ror.at[me], [*far, sec])
+    sent.append((others(ror), 9))
+    for p in [*far, sec]:
+        part = lax.dot_general(key_grad, wk[features(p), :], COLS, preferred_element_type=F32)
+        part += lax.dot_general(value_grad, wv[features(p), :], COLS, preferred_element_type=F32)
+        egb[pl.ds(p * N, N)] = part.astype(BF16).reshape(N, tt, F)
+        to_everyone(10, lambda s, n: egb.at[s * N + n], er.at[me], [p])
+    sent.append((others(egb), 10))
+    er[me] = egb[me]
+    for h in range(heads):
+        cols = slice(h * HEAD, (h + 1) * HEAD)
+        qg_out[:, cols] = product(dsc[h], keys[:, cols])
+    with mark("eg"):
+        arrive(others(ror), rsem.at[9])
+        arrive(others(er), rsem.at[10])
+    inner = to_column(jnp.sum(ror[...], axis=0), tt, ten * tt)
+    grad = jnp.sum(er[...].astype(F32), axis=0)
+    outer_grad = inv_o * (fg[...] * grad) - outer * (inv_o * inv_o * inner / D)
+    oall[ten] = outer_grad.astype(BF16)
+    to_tensor(11, lambda p: oall.at[ten], oall.at[ten], others(oall))
+    with mark("oall"):
+        arrive(others(oall), rsem.at[11])
+    grads = oall[...].reshape(T, F)
+    for p in far:
+        s9[p] = lax.dot_general(
+            grads, wd[units(p), :], COLS, preferred_element_type=F32
+        ).astype(BF16)
+        send(s9.at[p], r9.at[sec], ssem.at[12], rsem.at[12], section=p)
+    sent.append((others(s9), 12))
+    act_grad = lax.dot_general(grads, wd[units(sec), :], COLS, preferred_element_type=F32)
+    for s in range(S):
+        dw_out[s * Hs : (s + 1) * Hs, :] = product(hid[s], grads)
+    with mark("s9"):
+        arrive(others(r9), rsem.at[12])
+    for k in near:
+        act_grad = act_grad + r9[section(k)].astype(F32)
+    aall[sec] = act_grad.astype(BF16)
+    to_section(13, lambda p: aall.at[sec], aall.at[sec], others(aall), psem.at[3, sec])
+    rir[sec] = to_row(jnp.sum(act_grad * comb[...], axis=1, keepdims=True), 0)
+    to_section(14, lambda p: rir.at[sec], rir.at[sec], others(rir))
+    with mark("af"):
+        arrive(af.at[pl.ds(0, S - 1), pl.ds(0, 1)], rsem.at[5])
+        arrive(af.at[pl.ds(0, S - 1), pl.ds(1, 3)], rsem.at[8])
+    part = None
+    for k in range(S):
+        p = section(k)
+        if k:
+            with mark(f"aall{k}"):
+                arrive(aall.at[p], psem.at[3, p])
+        act_grad = aall[p].astype(F32)
+        factors = af[p].reshape(2, T, Hs)
+        up_grad = (act_grad * factors[0].astype(F32)).astype(BF16)
+        gate_grad = (act_grad * factors[1].astype(F32)).astype(BF16)
+        up[p] = up_grad
+        gate[p] = gate_grad
+        more = lax.dot_general(gate_grad, wg[:, units(p)], COLS, preferred_element_type=F32)
+        more += lax.dot_general(up_grad, wu[:, units(p)], COLS, preferred_element_type=F32)
+        part = more if part is None else part + more
+    s11[...] = part.reshape(N, tt, F)
+    s11b[...] = part.astype(BF16).reshape(N, tt, F)
+    to_tensor(15, lambda p: s11b.at[p], r11.at[ten], others(s11b))
+    with mark("rir"):
+        arrive(others(rir), rsem.at[14])
+    rit[ten] = jnp.sum(rir[...], axis=0)
+    to_tensor(16, lambda p: rit.at[ten], rit.at[ten], others(rit))
+    for s in range(S):
+        cols = slice(s * Hs, (s + 1) * Hs)
+        gw_out[:, cols] = product(normed, gate[s])
+        uw_out[:, cols] = product(normed, up[s])
+    with mark("s11"):
+        arrive(others(r11), rsem.at[15])
+        arrive(others(rit), rsem.at[16])
+    hidden = xg[ten].astype(F32)
+    scaled_in = s11[ten]
+    for k in across:
+        scaled_in = scaled_in + r11[tensor(k)].astype(F32)
+    scaled_in = mg[...] * scaled_in
+    inner = to_column(jnp.sum(rit[...], axis=0), tt, ten * tt)
+    squares = to_column(jnp.sum(sqr[...], axis=0), tt, ten * tt)
+    inv_in = lax.rsqrt(squares / D + EPSILON)
+    hg_out[...] = outer_grad + inv_in * scaled_in - hidden * (inv_in * inv_in * inner / D)
+    with mark("end"):
+        for cover, lane in sent:
+            arrive(cover, ssem.at[lane])
+
+
+def write_kernel(*refs):
+    count = len(refs) // 2
+    sem = refs[-1]
+    copies = [
+        pltpu.make_async_copy(refs[i], refs[count + i], sem.at[i]) for i in range(count)
+    ]
+    for copy in copies:
+        copy.start()
+    for copy in copies:
+        copy.wait()
+
+
+def fast(
+    S, N, enc_hidden, mlp_gain, final_gain, w_gate, w_up, w_down, key_weight, value_weight,
+    queries, context_grad,
+):
+    tt, F = enc_hidden.shape
+    T = N * tt
+    H = w_gate.shape[1]
+    Hs = H // S
+    vmem = pl.BlockSpec(memory_space=pltpu.VMEM)
+    hbm = pl.BlockSpec(memory_space=pltpu.HBM)
+    shape = jax.ShapeDtypeStruct
+    dma = pltpu.SemaphoreType.DMA
+    wk, wv, q, c = key_weight[0], value_weight[0], queries[0], context_grad[0]
+    rows, width = q.shape
+    heads = width // HEAD
+    buf = lambda *dims: pltpu.VMEM(dims, BF16)
+    wide = lambda *dims: pltpu.VMEM(dims, F32)
+    scratch = [
+        wide(2, 1, F), buf(2, F, H), buf(H, F), buf(2, *wk.shape), buf(2, rows, width),
+        buf(N, tt, F),
+        wide(S, 1, LANES),
+        buf(S, 2, T, Hs),
+        buf(S, 2, T, Hs),
+        buf(S, T, Hs),
+        buf(S, 4, T // 2, Hs),
+        wide(T, Hs),
+        wide(N, tt, F),
+        buf(N, tt, F),
+        buf(N, tt, F),
+        buf(S * N, tt, F),
+        wide(S * N, 1, LANES),
+        buf(S * N, tt, F),
+        buf(S * N, tt, F),
+        wide(S * N, 1, LANES),
+        buf(N, tt, F),
+        buf(S, T, Hs),
+        buf(S, T, Hs),
+        buf(S, T, Hs),
+        wide(S, 1, LANES),
+        buf(S, T, Hs),
+        buf(S, T, Hs),
+        wide(N, tt, F),
+        buf(N, tt, F),
+        buf(N, tt, F),
+        wide(N, 1, LANES),
+        buf(heads, T, rows),
+        dma((6,)), dma((17,)), dma((17,)), dma((4, S)),
+    ]
+    results = [
+        ((tt, F), F32), ((rows, width), BF16), ((F, H), BF16), ((F, H), BF16), ((H, F), BF16)
+    ]
+    made = pl.pallas_call(
+        functools.partial(chain_kernel, S, N),
+        out_shape=[pltpu.VMEM(*result) for result in results],
+        in_specs=[hbm] * 10,
+        out_specs=[vmem] * 5,
+        scratch_shapes=scratch,
+        compiler_params=pltpu.CompilerParams(
+            collective_id=0, has_side_effects=True, vmem_limit_bytes=CHAIN_VMEM_LIMIT
+        ),
+    )(enc_hidden, mlp_gain[None, :], final_gain[None, :], w_gate, w_up, w_down, wk, wv, q, c)
+    hidden_grad, query_grad, gate_grad, up_grad, down_grad = pl.pallas_call(
+        write_kernel,
+        out_shape=[shape(*result) for result in results],
+        in_specs=[vmem] * 5,
+        out_specs=[hbm] * 5,
+        scratch_shapes=[dma((5,))],
+        compiler_params=pltpu.CompilerParams(vmem_limit_bytes=WRITE_VMEM_LIMIT),
+    )(*made)
+    return query_grad[None, :, :], hidden_grad, gate_grad, up_grad, down_grad
+
+
+def on_device(S, N, enc_hidden, mlp_gain, final_gain, w_gate, *rest):
+    tt, F = enc_hidden.shape
+    Hs = w_gate.shape[1] // S
+    fits = Hs % LANES == 0 and F % LANES == 0 and tt % 16 == 0 and N * tt <= LANES
+    run = fast if fits else general
+    return run(S, N, enc_hidden, mlp_gain, final_gain, w_gate, *rest)
+
+
 def solution(mesh):
     in_specs = (
         P(("dp", "tensor"), "section"),

time: 94.9 us -> 76.5 us (0.81)
  Pallas kernels: 84.8 us -> 75.7 us
  matrix products: 7.19 us -> 0 us
  local copies, waits for them, and re-layouts: 1.96 us -> 0 us
    pallas_call x1 -> x2, Pallas kernels: 84.8 us -> 75.7 us  [the longest x1 72.3 us: fast(): pl.pallas_call(functools.partial(chain_kernel, S, N), out_shape=[pltpu.VM...]
    dot_general x3 -> x0, matrix products: 7.19 us -> none  [on_device(): lax.dot_general(a, b, ROWS, preferred_element_type=F32).astype(BF16)]
    unnamed x14 -> x0, local copies, waits for them, and re-layouts: 1.96 us -> none
where the time goes in v2:
time: 76.5 us; the launch traced here: 76.3 us
  Pallas kernels  75.7 us (99%)
    pallas_call x1, Pallas kernels, fast(): pl.pallas_call(functools.partial(chain_kernel, S, N), out_shape=[pltpu.VM...  72.3 us
    pallas_call x1, Pallas kernels, fast(): pl.pallas_call(write_kernel, out_shape=[shape(*result) for result in resu...  3.39 us

profile of v2, /device:TPU:0, one launch (start us, length us, event | category | flops | bytes accessed | tf_op | source)
XLA Modules:
  0.0 76.3 jit_solution(13533516715908564123)
XLA Ops:
  0.6 72.3 %shard_map.137 = (f32[16,512]{1,0:T(8,128)S(1)}, bf16[1024,1024]{1,0:T(8,128)(2,1)S(1)}, bf16[512,2048]{1,0:T(8,128)(2,1)S(1)}, bf16[512,2048]{1,0:T(8,128)(2,1)S(1)}, bf16[2048,512]{1,0:T(8,128)(2,1)S(1)}) custom-call(bf16[16,512]{1,0:T(8,128)(2,1)} %x_hbm.1, f32[1,512]{1,0:T(1,128)} %bitcast.11, f32[1,512]{1,0:T(1,128)} %bitcast.12, ...), custom_call_target="tpu_custom_call" | custom-call | tf_op jit(solution)/shard_map/pallas_call | solution.py:735
  72.9 3.4 %shard_map.138 = (f32[16,512]{1,0:T(8,128)}, bf16[1024,1024]{1,0:T(8,128)(2,1)}, bf16[512,2048]{1,0:T(8,128)(2,1)}, bf16[512,2048]{1,0:T(8,128)(2,1)}, bf16[2048,512]{1,0:T(8,128)(2,1)}) custom-call(f32[16,512]{1,0:T(8,128)S(1)} %get-tuple-element.15.refs_0_, bf16[1024,1024]{1,0:T(8,128)(2,1)S(1)} %get-tuple-element.16.refs_1_, ...), custom_call_target="tpu_custom_call" | custom-call | tf_op jit(solution)/shard_map/pallas_call | solution.py:745

commit v3 on v2

--- a/solution.py
+++ b/solution.py
@@ -371,7 +371,7 @@
     S, N, x_hbm, mg_hbm, fg_hbm, wg_hbm, wu_hbm, wd_hbm, wk_hbm, wv_hbm, q_hbm, c_hbm,
     hg_out, qg_out, gw_out, uw_out, dw_out,
     gains, wgu, wd, wkv, qc,
-    xg, sqr, gus, gur, hid, af, comb, ds, dsb, dr, encb, sso, egb, er, ror, oall,
+    xg, sqr, gus, gur, hold, stage, joined, hid, af, comb, ds, dsb, dr, encb, sso, egb, er, ror, oall,
     s9, r9, aall, rir, gate, up, s11, s11b, r11, rit, dsc,
     load_sem, ssem, rsem, psem,
 ):
@@ -398,6 +398,9 @@
     def distant(i):
         other = S - 1 - i - (i + rank) // (S - 1)
         return low * (S - 1) + turn * other
+
+    def place(y):
+        return low * (S - 1) + turn * y
 
     near = range(1, S)
     far = [distant(i) for i in range(S - 1)]
@@ -471,22 +474,59 @@
     square = jnp.sum(wide * wide, axis=1, keepdims=True)
     sqr[sec] = to_row(square, 0)
     to_section(1, lambda p: sqr.at[sec], sqr.at[sec], others(sqr))
-    for p in far:
-        gus[p, 0] = jnp.dot(scaled, wg[:, units(p)], preferred_element_type=F32).astype(BF16)
-        gus[p, 1] = jnp.dot(scaled, wu[:, units(p)], preferred_element_type=F32).astype(BF16)
-        send(gus.at[p], gur.at[sec], ssem.at[2], rsem.at[2], section=p)
+    line = S == 4
+    for i, p in enumerate(far):
+        for side, weight in enumerate((wg, wu)):
+            part = jnp.dot(scaled, weight[:, units(p)], preferred_element_type=F32)
+            gus[p, side] = part.astype(BF16)
+            if line and i == 0:
+                hold[side] = part
+
+                @pl.when(rank == 0)
+                def _(p=p, side=side):
+                    send(
+                        gus.at[p, side], stage.at[side], ssem.at[2], psem.at[4, side],
+                        section=place(1),
+                    )
+
+        if not (line and i == 0):
+            send(gus.at[p], gur.at[sec], ssem.at[2], rsem.at[2], section=p)
     sent.append((others(gus), 2))
     for load in loads[6:]:
         load.start()
     gate_pre = jnp.dot(scaled, wg[:, units(sec)], preferred_element_type=F32)
     up_pre = jnp.dot(scaled, wu[:, units(sec)], preferred_element_type=F32)
+    if line:
+        end = place(S - 1)
+
+        @pl.when(rank == 0)
+        def _():
+            gur[end] = jnp.zeros(gur.shape[1:], BF16)
+
+        @pl.when(rank == 1)
+        def _():
+            for side in range(2):
+                with mark(f"stage{side}"):
+                    arrive(stage.at[side], psem.at[4, side])
+                joined[side] = (hold[side] + stage[side].astype(F32)).astype(BF16)
+                send(joined.at[side], gur.at[sec, side], ssem.at[2], rsem.at[2], section=end)
+
     with mark("sq"):
         arrive(others(sqr), rsem.at[1])
     inv = lax.rsqrt(to_column(jnp.sum(sqr[...], axis=0), T, 0) / D + EPSILON)
     normed = (wide * inv * mg[...]).astype(BF16)
     loads[5].wait()
     with mark("gu"):
-        arrive(others(gur), rsem.at[2])
+        if line:
+            @pl.when(rank == 0)
+            def _():
+                arrive(gur.at[pl.ds(0, S - 2)], rsem.at[2])
+
+            @pl.when(rank == 1)
+            def _():
+                arrive(others(gur), rsem.at[2])
+        else:
+            arrive(others(gur), rsem.at[2])
     for k in near:
         gate_pre = gate_pre + gur[section(k), 0].astype(F32)
         up_pre = up_pre + gur[section(k), 1].astype(F32)
@@ -704,6 +744,9 @@
         wide(S, 1, LANES),
         buf(S, 2, T, Hs),
         buf(S, 2, T, Hs),
+        wide(2, T, Hs),
+        buf(2, T, Hs),
+        buf(2, T, Hs),
         buf(S, T, Hs),
         buf(S, 4, T // 2, Hs),
         wide(T, Hs),
@@ -727,7 +770,7 @@
         buf(N, tt, F),
         wide(N, 1, LANES),
         buf(heads, T, rows),
-        dma((6,)), dma((17,)), dma((17,)), dma((4, S)),
+        dma((6,)), dma((17,)), dma((17,)), dma((5, S)),
     ]
     results = [
         ((tt, F), F32), ((rows, width), BF16), ((F, H), BF16), ((F, H), BF16), ((H, F), BF16)

time: 76.5 us -> 74.3 us (0.971)
  Pallas kernels: 75.7 us -> 73.4 us
    pallas_call x1, Pallas kernels: 72.3 us -> 70.1 us  [fast(): pl.pallas_call(functools.partial(chain_kernel, S, N), out_shape=[pltpu.VM...]
where the time goes in v3:
time: 74.3 us; the launch traced here: 74.1 us
  Pallas kernels  73.4 us (99%)
    pallas_call x1, Pallas kernels, fast(): pl.pallas_call(functools.partial(chain_kernel, S, N), out_shape=[pltpu.VM...  70.1 us
    pallas_call x1, Pallas kernels, fast(): pl.pallas_call(write_kernel, out_shape=[shape(*result) for result in resu...  3.39 us

profile of v3, /device:TPU:0, one launch (start us, length us, event | category | flops | bytes accessed | tf_op | source)
XLA Modules:
  0.0 74.1 jit_solution(18143570287031603915)
XLA Ops:
  0.6 70.1 %shard_map.137 = (f32[16,512]{1,0:T(8,128)S(1)}, bf16[1024,1024]{1,0:T(8,128)(2,1)S(1)}, bf16[512,2048]{1,0:T(8,128)(2,1)S(1)}, bf16[512,2048]{1,0:T(8,128)(2,1)S(1)}, bf16[2048,512]{1,0:T(8,128)(2,1)S(1)}) custom-call(bf16[16,512]{1,0:T(8,128)(2,1)} %x_hbm.1, f32[1,512]{1,0:T(1,128)} %bitcast.11, f32[1,512]{1,0:T(1,128)} %bitcast.12, ...), custom_call_target="tpu_custom_call" | custom-call | tf_op jit(solution)/shard_map/pallas_call | solution.py:778
  70.7 3.4 %shard_map.138 = (f32[16,512]{1,0:T(8,128)}, bf16[1024,1024]{1,0:T(8,128)(2,1)}, bf16[512,2048]{1,0:T(8,128)(2,1)}, bf16[512,2048]{1,0:T(8,128)(2,1)}, bf16[2048,512]{1,0:T(8,128)(2,1)}) custom-call(f32[16,512]{1,0:T(8,128)S(1)} %get-tuple-element.15.refs_0_, bf16[1024,1024]{1,0:T(8,128)(2,1)S(1)} %get-tuple-element.16.refs_1_, ...), custom_call_target="tpu_custom_call" | custom-call | tf_op jit(solution)/shard_map/pallas_call | solution.py:788

commit v4 on v3

--- a/solution.py
+++ b/solution.py
@@ -368,11 +368,11 @@
 
 
 def chain_kernel(
-    S, N, x_hbm, mg_hbm, fg_hbm, wg_hbm, wu_hbm, wd_hbm, wk_hbm, wv_hbm, q_hbm, c_hbm,
+    S, N, G, x_hbm, mg_hbm, fg_hbm, wg_hbm, wu_hbm, wd_hbm, wk_hbm, wv_hbm, q_hbm, c_hbm,
     hg_out, qg_out, gw_out, uw_out, dw_out,
     gains, wgu, wd, wkv, qc,
-    xg, sqr, gus, gur, hold, stage, joined, hid, af, comb, ds, dsb, dr, encb, sso, egb, er, ror, oall,
-    s9, r9, aall, rir, gate, up, s11, s11b, r11, rit, dsc,
+    xg, sqr, gus, gur, hold, stage, joined, hid, af, afg, comb, combg, ds, dsb, dr, encb, sso, egb, er, ror, oall, oallg,
+    s9, r9, aall, rir, gateg, upg, gate, up, s11b, r11, rits, rit, dsc,
     load_sem, ssem, rsem, psem,
 ):
     tt, F = x_hbm.shape
@@ -383,6 +383,7 @@
     heads = qc.shape[2] // HEAD
     sec = lax.axis_index("section")
     ten = lax.axis_index("tensor")
+    partner = lax.rem(lax.axis_index("dp") + 1, G)
     turn = 1 - 2 * (sec // ((S + 1) // 2))
     sent = []
 
@@ -446,6 +447,14 @@
                     device_id={"section": section(k), "tensor": tensor(j)},
                     device_id_type=MESH,
                 )
+    crossed = [(p, ten) for p in [sec, *far]] + [(sec, tensor(j)) for j in across]
+    for p, n in crossed:
+        pl.semaphore_signal(
+            barrier,
+            inc=1,
+            device_id={"section": p, "tensor": n, "dp": partner},
+            device_id_type=MESH,
+        )
     loads = [
         pltpu.make_async_copy(src, dst, load_sem.at[i])
         for src, dst, i in (
@@ -459,7 +468,7 @@
         load.start()
     loads[0].wait()
     with mark("enter"):
-        pl.semaphore_wait(barrier, S * N - 1)
+        pl.semaphore_wait(barrier, S * N - 1 + len(crossed))
     to_tensor(0, lambda p: xg.at[ten], xg.at[ten], others(xg))
     arrive(gains, load_sem.at[1])
     arrive(wgu, load_sem.at[2])
@@ -538,11 +547,13 @@
     to_section(3, lambda p: hid.at[sec], hid.at[sec], others(hid), psem.at[0, sec])
     factor = up_pre * (sig * (1.0 + gate_pre * (1.0 - sig)))
     piece = T // 2
-    af[sec, 0] = act[:piece].astype(BF16)
-    af[sec, 1] = act[piece:].astype(BF16)
-    af[sec, 2] = factor[:piece].astype(BF16)
-    af[sec, 3] = factor[piece:].astype(BF16)
+    af[0] = act[:piece].astype(BF16)
+    af[1] = act[piece:].astype(BF16)
+    af[2] = factor[:piece].astype(BF16)
+    af[3] = factor[piece:].astype(BF16)
     comb[...] = act * up_pre + factor * gate_pre
+    send(comb, combg, ssem.at[17], rsem.at[17], dp=partner)
+    sent.append((comb, 17))
     down = jnp.dot(hid[sec], wd[units(sec), :], preferred_element_type=F32)
     for k in near:
         p = section(k)
@@ -552,9 +563,17 @@
     ds[...] = down.reshape(N, tt, F)
     dsb[...] = down.astype(BF16).reshape(N, tt, F)
     to_tensor(4, lambda p: dsb.at[p], dr.at[ten], others(dsb))
-    early = lambda p: af.at[p, pl.ds(0, 1)]
-    late = lambda p: af.at[p, pl.ds(1, 3)]
-    to_section(5, lambda p: early(sec), early(sec), af.at[pl.ds(0, S - 1), pl.ds(0, 1)])
+    early, late = pl.ds(0, 1), pl.ds(1, 3)
+
+    def share_factors(lane, pieces):
+        for p in [*far, sec]:
+            send(
+                af.at[pieces], afg.at[sec, pieces], ssem.at[lane], rsem.at[lane],
+                section=p, dp=partner,
+            )
+        sent.append((afg.at[:, pieces], lane))
+
+    share_factors(5, early)
     with mark("ds"):
         arrive(others(dr), rsem.at[4])
     outer = xg[ten].astype(F32) + ds[ten]
@@ -579,7 +598,7 @@
                 tensor=tensor(j),
             )
     sent.append((others(encb), 7))
-    to_section(8, lambda p: late(sec), late(sec), af.at[pl.ds(0, S - 1), pl.ds(1, 3)])
+    share_factors(8, late)
     arrive(wkv, load_sem.at[4])
     arrive(qc, load_sem.at[5])
     keys = values = None
@@ -642,10 +661,15 @@
     grad = jnp.sum(er[...].astype(F32), axis=0)
     outer_grad = inv_o * (fg[...] * grad) - outer * (inv_o * inv_o * inner / D)
     oall[ten] = outer_grad.astype(BF16)
+    for k in range(N):
+        send(
+            oall.at[ten], oallg.at[ten], ssem.at[18], rsem.at[18], tensor=tensor(k), dp=partner
+        )
+    sent.append((oall, 18))
     to_tensor(11, lambda p: oall.at[ten], oall.at[ten], others(oall))
     with mark("oall"):
-        arrive(others(oall), rsem.at[11])
-    grads = oall[...].reshape(T, F)
+        arrive(oallg, rsem.at[18])
+    grads = oallg[...].reshape(T, F)
     for p in far:
         s9[p] = lax.dot_general(
             grads, wd[units(p), :], COLS, preferred_element_type=F32
@@ -653,6 +677,8 @@
         send(s9.at[p], r9.at[sec], ssem.at[12], rsem.at[12], section=p)
     sent.append((others(s9), 12))
     act_grad = lax.dot_general(grads, wd[units(sec), :], COLS, preferred_element_type=F32)
+    arrive(others(oall), rsem.at[11])
+    grads = oall[...].reshape(T, F)
     for s in range(S):
         dw_out[s * Hs : (s + 1) * Hs, :] = product(hid[s], grads)
     with mark("s9"):
@@ -661,11 +687,12 @@
         act_grad = act_grad + r9[section(k)].astype(F32)
     aall[sec] = act_grad.astype(BF16)
     to_section(13, lambda p: aall.at[sec], aall.at[sec], others(aall), psem.at[3, sec])
-    rir[sec] = to_row(jnp.sum(act_grad * comb[...], axis=1, keepdims=True), 0)
+    arrive(combg, rsem.at[17])
+    rir[sec] = to_row(jnp.sum(act_grad * combg[...], axis=1, keepdims=True), 0)
     to_section(14, lambda p: rir.at[sec], rir.at[sec], others(rir))
     with mark("af"):
-        arrive(af.at[pl.ds(0, S - 1), pl.ds(0, 1)], rsem.at[5])
-        arrive(af.at[pl.ds(0, S - 1), pl.ds(1, 3)], rsem.at[8])
+        arrive(afg.at[:, early], rsem.at[5])
+        arrive(afg.at[:, late], rsem.at[8])
     part = None
     for k in range(S):
         p = section(k)
@@ -673,33 +700,40 @@
             with mark(f"aall{k}"):
                 arrive(aall.at[p], psem.at[3, p])
         act_grad = aall[p].astype(F32)
-        factors = af[p].reshape(2, T, Hs)
+        factors = afg[p].reshape(2, T, Hs)
         up_grad = (act_grad * factors[0].astype(F32)).astype(BF16)
         gate_grad = (act_grad * factors[1].astype(F32)).astype(BF16)
-        up[p] = up_grad
-        gate[p] = gate_grad
+        upg[p] = up_grad
+        gateg[p] = gate_grad
+        send(upg.at[p], up.at[p], ssem.at[19], rsem.at[19], dp=partner)
+        send(gateg.at[p], gate.at[p], ssem.at[20], rsem.at[20], dp=partner)
         more = lax.dot_general(gate_grad, wg[:, units(p)], COLS, preferred_element_type=F32)
         more += lax.dot_general(up_grad, wu[:, units(p)], COLS, preferred_element_type=F32)
         part = more if part is None else part + more
-    s11[...] = part.reshape(N, tt, F)
+    sent += [(upg, 19), (gateg, 20)]
     s11b[...] = part.astype(BF16).reshape(N, tt, F)
-    to_tensor(15, lambda p: s11b.at[p], r11.at[ten], others(s11b))
+    for k in [*across, 0]:
+        p = tensor(k)
+        send(s11b.at[p], r11.at[ten], ssem.at[15], rsem.at[15], tensor=p, dp=partner)
+    sent.append((s11b, 15))
     with mark("rir"):
         arrive(others(rir), rsem.at[14])
-    rit[ten] = jnp.sum(rir[...], axis=0)
-    to_tensor(16, lambda p: rit.at[ten], rit.at[ten], others(rit))
+    rits[...] = jnp.sum(rir[...], axis=0)
+    for k in [*across, 0]:
+        send(rits, rit.at[ten], ssem.at[16], rsem.at[16], tensor=tensor(k), dp=partner)
+    sent.append((rit, 16))
+    with mark("gateup"):
+        arrive(up, rsem.at[19])
+        arrive(gate, rsem.at[20])
     for s in range(S):
         cols = slice(s * Hs, (s + 1) * Hs)
         gw_out[:, cols] = product(normed, gate[s])
         uw_out[:, cols] = product(normed, up[s])
     with mark("s11"):
-        arrive(others(r11), rsem.at[15])
-        arrive(others(rit), rsem.at[16])
+        arrive(r11, rsem.at[15])
+        arrive(rit, rsem.at[16])
     hidden = xg[ten].astype(F32)
-    scaled_in = s11[ten]
-    for k in across:
-        scaled_in = scaled_in + r11[tensor(k)].astype(F32)
-    scaled_in = mg[...] * scaled_in
+    scaled_in = mg[...] * jnp.sum(r11[...].astype(F32), axis=0)
     inner = to_column(jnp.sum(rit[...], axis=0), tt, ten * tt)
     squares = to_column(jnp.sum(sqr[...], axis=0), tt, ten * tt)
     inv_in = lax.rsqrt(squares / D + EPSILON)
@@ -722,7 +756,7 @@
 
 
 def fast(
-    S, N, enc_hidden, mlp_gain, final_gain, w_gate, w_up, w_down, key_weight, value_weight,
+    S, N, G, enc_hidden, mlp_gain, final_gain, w_gate, w_up, w_down, key_weight, value_weight,
     queries, context_grad,
 ):
     tt, F = enc_hidden.shape
@@ -748,7 +782,9 @@
         buf(2, T, Hs),
         buf(2, T, Hs),
         buf(S, T, Hs),
+        buf(4, T // 2, Hs),
         buf(S, 4, T // 2, Hs),
+        wide(T, Hs),
         wide(T, Hs),
         wide(N, tt, F),
         buf(N, tt, F),
@@ -759,24 +795,27 @@
         buf(S * N, tt, F),
         wide(S * N, 1, LANES),
         buf(N, tt, F),
+        buf(N, tt, F),
         buf(S, T, Hs),
         buf(S, T, Hs),
         buf(S, T, Hs),
         wide(S, 1, LANES),
         buf(S, T, Hs),
         buf(S, T, Hs),
-        wide(N, tt, F),
+        buf(S, T, Hs),
+        buf(S, T, Hs),
         buf(N, tt, F),
         buf(N, tt, F),
+        wide(1, LANES),
         wide(N, 1, LANES),
         buf(heads, T, rows),
-        dma((6,)), dma((17,)), dma((17,)), dma((5, S)),
+        dma((6,)), dma((21,)), dma((21,)), dma((5, S)),
     ]
     results = [
         ((tt, F), F32), ((rows, width), BF16), ((F, H), BF16), ((F, H), BF16), ((H, F), BF16)
     ]
     made = pl.pallas_call(
-        functools.partial(chain_kernel, S, N),
+        functools.partial(chain_kernel, S, N, G),
         out_shape=[pltpu.VMEM(*result) for result in results],
         in_specs=[hbm] * 10,
         out_specs=[vmem] * 5,
@@ -796,12 +835,12 @@
     return query_grad[None, :, :], hidden_grad, gate_grad, up_grad, down_grad
 
 
-def on_device(S, N, enc_hidden, mlp_gain, final_gain, w_gate, *rest):
+def on_device(S, N, G, enc_hidden, mlp_gain, final_gain, w_gate, *rest):
     tt, F = enc_hidden.shape
     Hs = w_gate.shape[1] // S
     fits = Hs % LANES == 0 and F % LANES == 0 and tt % 16 == 0 and N * tt <= LANES
-    run = fast if fits else general
-    return run(S, N, enc_hidden, mlp_gain, final_gain, w_gate, *rest)
+    run = functools.partial(fast, S, N, G) if fits and G == 2 else functools.partial(general, S, N)
+    return run(enc_hidden, mlp_gain, final_gain, w_gate, *rest)
 
 
 def solution(mesh):
@@ -824,7 +863,8 @@
         P(("dp", "section"), "tensor"),
         P(("dp", "tensor"), "section"),
     )
-    body = functools.partial(on_device, mesh.shape["section"], mesh.shape["tensor"])
+    sizes = [mesh.shape[axis] for axis in ("section", "tensor", "dp")]
+    body = functools.partial(on_device, *sizes)
     return jax.shard_map(
         body, mesh=mesh, in_specs=in_specs, out_specs=out_specs, check_vma=False
     )

time: 74.3 us -> 72 us (0.969)
  Pallas kernels: 73.4 us -> 71.1 us
    pallas_call x1, Pallas kernels: 70.1 us -> 67.7 us  [fast(): pl.pallas_call(functools.partial(chain_kernel, S, N, G), out_shape=[pltpu...]
where the time goes in v4:
time: 72 us; the launch traced here: 71.7 us
  Pallas kernels  71.1 us (99%)
    pallas_call x1, Pallas kernels, fast(): pl.pallas_call(functools.partial(chain_kernel, S, N, G), out_shape=[pltpu...  67.7 us
    pallas_call x1, Pallas kernels, fast(): pl.pallas_call(write_kernel, out_shape=[shape(*result) for result in resu...  3.39 us

profile of v4, /device:TPU:0, one launch (start us, length us, event | category | flops | bytes accessed | tf_op | source)
XLA Modules:
  0.0 71.7 jit_solution(16781587392577927729)
XLA Ops:
  0.6 67.7 %shard_map.137 = (f32[16,512]{1,0:T(8,128)S(1)}, bf16[1024,1024]{1,0:T(8,128)(2,1)S(1)}, bf16[512,2048]{1,0:T(8,128)(2,1)S(1)}, bf16[512,2048]{1,0:T(8,128)(2,1)S(1)}, bf16[2048,512]{1,0:T(8,128)(2,1)S(1)}) custom-call(bf16[16,512]{1,0:T(8,128)(2,1)} %x_hbm.1, f32[1,512]{1,0:T(1,128)} %bitcast.11, f32[1,512]{1,0:T(1,128)} %bitcast.12, ...), custom_call_target="tpu_custom_call" | custom-call | tf_op jit(solution)/shard_map/pallas_call | solution.py:817
  68.3 3.4 %shard_map.138 = (f32[16,512]{1,0:T(8,128)}, bf16[1024,1024]{1,0:T(8,128)(2,1)}, bf16[512,2048]{1,0:T(8,128)(2,1)}, bf16[512,2048]{1,0:T(8,128)(2,1)}, bf16[2048,512]{1,0:T(8,128)(2,1)}) custom-call(f32[16,512]{1,0:T(8,128)S(1)} %get-tuple-element.15.refs_0_, bf16[1024,1024]{1,0:T(8,128)(2,1)S(1)} %get-tuple-element.16.refs_1_, ...), custom_call_target="tpu_custom_call" | custom-call | tf_op jit(solution)/shard_map/pallas_call | solution.py:827

commit v5 on v4

--- a/solution.py
+++ b/solution.py
@@ -563,7 +563,7 @@
     ds[...] = down.reshape(N, tt, F)
     dsb[...] = down.astype(BF16).reshape(N, tt, F)
     to_tensor(4, lambda p: dsb.at[p], dr.at[ten], others(dsb))
-    early, late = pl.ds(0, 1), pl.ds(1, 3)
+    early, late = pl.ds(0, 2), pl.ds(2, 2)
 
     def share_factors(lane, pieces):
         for p in [*far, sec]:

time: 72 us -> 72.8 us (1.011)
  Pallas kernels: 71.1 us -> 71.9 us
    pallas_call x1, Pallas kernels: 67.7 us -> 68.5 us  [fast(): pl.pallas_call(functools.partial(chain_kernel, S, N, G), out_shape=[pltpu...]
where the time goes in v5:
time: 72.8 us; the launch traced here: 72.5 us
  Pallas kernels  71.9 us (99%)
    pallas_call x1, Pallas kernels, fast(): pl.pallas_call(functools.partial(chain_kernel, S, N, G), out_shape=[pltpu...  68.5 us
    pallas_call x1, Pallas kernels, fast(): pl.pallas_call(write_kernel, out_shape=[shape(*result) for result in resu...  3.39 us

profile of v5, /device:TPU:0, one launch (start us, length us, event | category | flops | bytes accessed | tf_op | source)
XLA Modules:
  0.0 72.5 jit_solution(5748172584147677289)
XLA Ops:
  0.6 68.5 %shard_map.137 = (f32[16,512]{1,0:T(8,128)S(1)}, bf16[1024,1024]{1,0:T(8,128)(2,1)S(1)}, bf16[512,2048]{1,0:T(8,128)(2,1)S(1)}, bf16[512,2048]{1,0:T(8,128)(2,1)S(1)}, bf16[2048,512]{1,0:T(8,128)(2,1)S(1)}) custom-call(bf16[16,512]{1,0:T(8,128)(2,1)} %x_hbm.1, f32[1,512]{1,0:T(1,128)} %bitcast.11, f32[1,512]{1,0:T(1,128)} %bitcast.12, ...), custom_call_target="tpu_custom_call" | custom-call | tf_op jit(solution)/shard_map/pallas_call | solution.py:817
  69.1 3.4 %shard_map.138 = (f32[16,512]{1,0:T(8,128)}, bf16[1024,1024]{1,0:T(8,128)(2,1)}, bf16[512,2048]{1,0:T(8,128)(2,1)}, bf16[512,2048]{1,0:T(8,128)(2,1)}, bf16[2048,512]{1,0:T(8,128)(2,1)}) custom-call(f32[16,512]{1,0:T(8,128)S(1)} %get-tuple-element.15.refs_0_, bf16[1024,1024]{1,0:T(8,128)(2,1)S(1)} %get-tuple-element.16.refs_1_, ...), custom_call_target="tpu_custom_call" | custom-call | tf_op jit(solution)/shard_map/pallas_call | solution.py:827
